TPU v7x, 128 devices: a whole 4x4x4 slice. The times are simulated.
128 devices in a mesh: gx: 8 (over x, core), gy: 16 (over z, y).
Axes of the slice: x: 4, y: 4, z: 4, core: 2. Of those that a mesh axis runs over, the one named last changes fastest.
Arguments:
- atm_fields: bfloat16 [786432, 128], P(('gx', 'gy')), may hold values from -6 to 6
- atm_pos: int32 [3072], replicated, may hold values from 0 to 3071, as said below
- tile_src: int32 [20480], P(('gx', 'gy')), may hold values from 0 to 3071, as said below
- tile_tgt: int32 [20480], P(('gx', 'gy')), may hold values from 0 to 1
- tile_count: int32 [128], P(('gx', 'gy')), may hold values from 128 to 160, as said below
- tile_weight: bfloat16 [20480, 256, 256], P(('gx', 'gy')), may hold values from -0.0625 to 0.0625
- ocean_state: bfloat16 [256, 256, 128], P('gy', 'gx'), may hold values from -6 to 6
- land_mask: int32 [256, 256], P('gy', 'gx'), may hold values 0 or 1
- mixing: float32 [128], replicated, may hold values from 0.03 to 0.24
Outputs:
- ocean_next: bfloat16 [256, 256, 128], P('gy', 'gx')
Inputs may be any that keep to these rules, and one draw needn't show every extreme that they name: `atm_pos`: a permutation of the block positions. `tile_src`: among the 160 slots of one device, live or not, no owning device (atm_pos of the block // 24) is named by more than 2 slots; on every device with 160 live slots some owner is named by exactly 2. `tile_count`: live slots are a device's first ones; one device has exactly 160.
All inputs are finite; a program needn't handle non-finite values. No bound on the sum of `land_mask` on one device may be relied on, other than what follows from the above.
Results may differ from a plain program's by a relative error of at most 0.001.
Values may be sent and summed in bfloat16 or wider, within the bound.
A program may use at most 128 MiB of HBM per device.

v0:
```python
import jax
import jax.numpy as jnp
from jax import lax
from jax.sharding import PartitionSpec as P

RECV_SLOTS = 256


def padded(shard, sides, width, wrap):
    for axis, dim in sides:
        size, length = (lax.axis_size(axis), shard.shape[dim])
        up = [(i, (i + 1) % size) for i in range(size if wrap else size - 1)]
        down = [(j, i) for i, j in up]
        last = lax.slice_in_dim(shard, length - width, length, axis=dim)
        leading = lax.slice_in_dim(shard, 0, width, axis=dim)
        before = lax.ppermute(last, axis, up)
        after = lax.ppermute(leading, axis, down)
        shard = jnp.concatenate([before, shard, after], axis=dim)
    return shard


def partner(value, axis, distance):
    mask = 2**distance
    pairs = [(source, source ^ mask) for source in range(lax.axis_size(axis))]
    return lax.ppermute(value, axis, pairs)


def plan_tiles(sources, tile_live, atm_pos, block_count):
    positions = atm_pos[sources]
    owners = positions // block_count
    local_slot = positions % block_count
    ordinal = jnp.arange(sources.shape[0], dtype=jnp.int32)
    active = ordinal < tile_live
    earlier = (
        (owners[:, None] == owners[None, :])
        & active[None, :]
        & (ordinal[None, :] < ordinal[:, None])
    )
    order_rank = jnp.sum(earlier.astype(jnp.int32), axis=1)
    return (owners, order_rank, local_slot, active)


def local(
    atm_fields, atm_pos, tile_src, tile_tgt, tile_count, tile_weight, ocean_state, land_mask, mixing
):
    block_rows = tile_weight.shape[1]
    tiles = tile_weight.shape[0]
    channels = atm_fields.shape[1]
    block_count = atm_fields.shape[0] // block_rows
    devices = lax.axis_size("gx") * lax.axis_size("gy")
    per_peer = RECV_SLOTS // devices
    owners, order_rank, local_slot, active = plan_tiles(
        tile_src, tile_count[0], atm_pos, block_count
    )
    slots_flat = jnp.arange(RECV_SLOTS, dtype=jnp.int32)
    wanted_slot = owners * per_peer + order_rank
    matches = (wanted_slot[None, :] == slots_flat[:, None]) & active[None, :]
    asking = jnp.sum(jnp.where(matches, local_slot[None, :] + 1, 0), axis=1)
    requests = lax.all_to_all(
        asking.reshape(devices, per_peer), ("gx", "gy"), split_axis=0, concat_axis=0, tiled=True
    )
    wanted = requests.reshape(RECV_SLOTS)
    block_table = atm_fields.reshape(block_count, block_rows, channels)
    outgoing = jnp.where(
        (wanted > 0)[:, None, None],
        block_table[jnp.maximum(wanted - 1, 0)],
        jnp.zeros((), jnp.bfloat16),
    )
    outgoing = outgoing.reshape(devices, per_peer, block_rows, channels)
    arrived = lax.all_to_all(outgoing, ("gx", "gy"), split_axis=0, concat_axis=0, tiled=True)
    arrived = arrived.reshape(RECV_SLOTS, block_rows, channels)
    lat_rows = ocean_state.shape[0]
    lon_cols = ocean_state.shape[1]
    target_blocks = lat_rows * lon_cols // block_rows
    slots = jnp.where(active, owners * per_peer + order_rank, 0)
    select = (
        (tile_tgt[:, None] == jnp.arange(target_blocks, dtype=jnp.int32)[None, :]) & active[:, None]
    ).astype(jnp.float32)
    group_size = max((divisor for divisor in range(1, 33) if tiles % divisor == 0))
    groups = tiles // group_size

    def advance(running, pieces):
        weights, group_slots, group_select = pieces
        gathered = arrived[group_slots]
        partial_sum = jnp.einsum(
            "tij,tjc->tic", weights, gathered, preferred_element_type=jnp.float32
        )
        added = jnp.einsum(
            "tb,tic->bic", group_select, partial_sum, precision=lax.Precision.HIGHEST
        )
        return (running + added, None)

    starting = jnp.zeros((target_blocks, block_rows, channels), jnp.float32)
    remapped = lax.scan(
        advance,
        starting,
        (
            tile_weight.reshape(groups, group_size, block_rows, block_rows),
            slots.reshape(groups, group_size),
            select.reshape(groups, group_size, target_blocks),
        ),
    )[0]
    forcing = remapped.reshape(lat_rows, lon_cols, channels)
    mask_half = land_mask.astype(jnp.bfloat16)
    lon_state, lon_mask = (
        padded(ocean_state, (("gx", 1),), 1, True),
        padded(mask_half, (("gx", 1),), 1, True),
    )
    lat_state, lat_mask = (
        padded(ocean_state, (("gy", 0),), 1, False),
        padded(mask_half, (("gy", 0),), 1, False),
    )
    fold_state = jnp.flip(ocean_state[-1], 0)
    fold_mask = jnp.flip(mask_half[-1], 0)
    for bit_number in range(lax.axis_size("gx").bit_length() - 1):
        fold_state, fold_mask = partner((fold_state, fold_mask), "gx", bit_number)
    is_top = lax.axis_index("gy") == lax.axis_size("gy") - 1
    north_state = jnp.concatenate(
        [lat_state[2:-1], jnp.where(is_top, fold_state, lat_state[-1])[None]], axis=0
    )
    north_mask = jnp.concatenate(
        [lat_mask[2:-1], jnp.where(is_top, fold_mask, lat_mask[-1])[None]], axis=0
    )
    center = ocean_state.astype(jnp.float32)
    sides = (
        (lon_state[:, :-2], lon_mask[:, :-2]),
        (lon_state[:, 2:], lon_mask[:, 2:]),
        (lat_state[:-2], lat_mask[:-2]),
        (north_state, north_mask),
    )
    diffusion = jnp.zeros_like(center)
    for side_state, side_mask in sides:
        diffusion = diffusion + side_mask.astype(jnp.float32)[..., None] * (
            side_state.astype(jnp.float32) - center
        )
    result = mask_half.astype(jnp.float32)[..., None] * (center + forcing + mixing * diffusion)
    return result.astype(jnp.bfloat16)


def solution(mesh):
    in_specs = (
        P(("gx", "gy"), None),
        P(),
        P(("gx", "gy")),
        P(("gx", "gy")),
        P(("gx", "gy")),
        P(("gx", "gy"), None, None),
        P("gy", "gx", None),
        P("gy", "gx"),
        P(),
    )
    out_specs = P("gy", "gx", None)
    return jax.shard_map(local, mesh=mesh, in_specs=in_specs, out_specs=out_specs, check_vma=False)
```

profile of v0, /device:TPU:74, one launch (start us, length us, event | category | flops | bytes accessed | tf_op | source)
XLA Modules:
  0.0 409.2 jit_solution(2369855762100745648)
XLA Ops:
  0.0 0.8 compare_select_fusion.1
  0.8 1.9 gather_fusion.1
  3.4 0.2 convert_reduce_fusion
  3.6 0.1 select_reduce_fusion
  3.8 0.1 all_to_all.9
  3.9 15.6 %all_to_all.14 = s32[128,1,2]{2,1,0:T(1,128)S(1)} all-to-all(s32[128,1,2]{2,1,0:T(1,128)S(1)} %bitcast.58), channel_id=1, replica_groups=mesh['gx'=8,'gy'=16] {'gx','gy'}, dimensions={0} | all-to-all | bytes 2048 | tf_op jit(solution)/shard_map/all_to_all | solution.py:59
  19.6 0.1 copy.30
  19.7 0.1 reshape.189
  19.9 0.1 copy.28
  20.0 9.6 %gather_fusion.2 = bf16[256,256,128]{2,1,0:T(8,128)(2,1)} fusion(bf16[24,256,128]{2,1,0:T(8,128)(2,1)S(1)} %bitcast.54, s32[1024]{0:T(1024)S(1)} %pad_clamp_fusion.1), kind=kCustom, calls=%fused_computation.2 | custom fusion | bytes 33555456 | tf_op jit(solution)/shard_map/gather | solution.py:66
  29.6 14.0 %broadcast_select_fusion = bf16[128,2,256,128]{3,2,1,0:T(8,128)(2,1)} fusion(bf16[128,2,256,128]{3,2,1,0:T(8,128)(2,1)} %bitcast.55, pred[128,2]{1,0:T(8,128)(4,1)S(1)} %copy.28), kind=kLoop, calls=%fused_computation.18 | loop fusion | flops 8388608 | bytes 33554688 | tf_op jit(solution)/shard_map/jit(_where)/select_n | solution.py:64
  43.6 9.8 %all-to-all-start.1 = ((bf16[128,2,256,128]{3,2,1,0:T(8,128)(2,1)}), bf16[128,2,256,128]{3,2,1,0:T(8,128)(2,1)}, u32[]{:S(2)}, u32[]{:S(2)}) async-start(bf16[128,2,256,128]{3,2,1,0:T(8,128)(2,1)} %broadcast_select_fusion), calls=%async_computation.1 | async-start | bytes 33554432 | tf_op jit(solution)/shard_map/all_to_all | solution.py:70
  53.5 3.4 collective-permute-start.4
  57.0 1.7 collective-permute-start.2
  58.7 0.1 rev.8
  58.9 2.4 collective-permute-start.9
  61.3 0.1 reduce_sum.21
  61.4 0.1 div.22
  61.4 0.1 and.59
  61.5 0.1 eq.47
  61.7 214.6 %collective-permute-done = bf16[16,1]{1,0:T(8,128)(2,1)S(1)} collective-permute-done((bf16[16,1]{1,0:T(8,128)(2,1)S(1)}, bf16[16,1]{1,0:T(8,128)(2,1)S(1)}, u32[]{:S(2)}, u32[]{:S(2)}) %collective-permute-start) | collective-permute-done | bytes 64 | tf_op jit(solution)/shard_map/ppermute | solution.py:16
  276.3 1.9 collective-permute-start.13
  278.2 3.9 collective-permute-start.5
  282.1 0.1 collective-permute-start.7
  282.2 0.1 fusion.33
  282.3 3.5 collective-permute-done.7
  285.8 5.1 %collective-permute-done.8 = bf16[32]{0:T(256)(128)(2,1)S(1)} collective-permute-done((bf16[32]{0:T(256)(128)(2,1)S(1)}, bf16[32]{0:T(256)(128)(2,1)S(1)}, u32[]{:S(2)}, u32[]{:S(2)}) %collective-permute-start.8) | collective-permute-done | bytes 96 | tf_op jit(solution)/shard_map/ppermute | solution.py:25
  290.9 3.6 collective-permute-done.11
  294.5 0.2 collective-permute-start.12
  294.7 4.9 %collective-permute-done.12 = bf16[32,128]{1,0:T(8,128)(2,1)S(1)} collective-permute-done((bf16[32,128]{1,0:T(8,128)(2,1)S(1)}, bf16[32,128]{1,0:T(8,128)(2,1)S(1)}, u32[]{:S(2)}, u32[]{:S(2)}) %collective-permute-start.12) | collective-permute-done | bytes 8224 | tf_op jit(solution)/shard_map/ppermute | solution.py:25
  299.7 108.1 %while.11 = (s32[]{:T(128)}, f32[2,256,128]{2,0,1:T(2,128)S(1)}, f32[5,32,2]{1,2,0:T(2,128)S(1)}, bf16[5,32,256,256]{3,2,1,0:T(8,128)(2,1)}, s32[5,32]{1,0:T(8,1...) while((s32[]{:T(128)}, f32[2,256,128]{2,0,1:T(2,128)S(1)}, ...), condition=%wide.region_3.4_spmd.clone, body=%wide.region_2.3_spmd.clone.sunk | while | flops 562168960 | bytes 19404904 | solution.py:94
  299.8 8.0 %gather_fusion = bf16[32,256,128]{2,1,0:T(8,128)(2,1)} fusion(bf16[256,256,128]{2,1,0:T(8,128)(2,1)} %get-tuple-element.148, s32[1024]{0:T(1024)S(1)} %pad_clamp_fusion.4), kind=kCustom, calls=%fused_computation.clone.clone.1 | custom fusion | bytes 4194432 | tf_op jit(solution)/shard_map/while/body/eval_jaxpr/gather | solution.py:84
  307.8 6.1 %fusion.54 = f32[32,256,128]{2,1,0:T(8,128)} fusion(bf16[32,256,128]{2,1,0:T(8,128)(2,1)} %gather_fusion, bf16[5,32,256,256]{3,2,1,0:T(8,128)(2,1)} %get-tuple-element.146, s32[]{:T(128)} %get-tuple-element.135), kind=kOutput, calls=%fused_computation.3.clone.1 | convolution fusion | flops 536870912 | bytes 10486272 | tf_op jit(solution)/shard_map/while/body/eval_jaxpr/tij,tjc->tic/dot_general | solution.py:85
  313.8 7.6 %fusion.55 = f32[2,256,128]{2,0,1:T(2,128)S(1)} fusion(f32[32,256,128]{2,1,0:T(8,128)} %fusion.54, f32[2,256,128]{2,0,1:T(2,128)S(1)} %get-tuple-element.136, pred[]{:T(512)S(6)} %compare.3, f32[5,32,2]{1,2,0:T(2,128)S(1)} %get-tuple-element.145, s32[]{:T(128)} %get-tuple-element.135), kind=kOutput, calls=%fused_computation.8.clone.1 | convolution fusion | flops 25296896 | bytes 4719621 | tf_op jit(solution)/shard_map/while/body/eval_jaxpr/tb,tic->bic/dot_general | solution.py:88
  321.4 7.9 %gather_fusion = bf16[32,256,128]{2,1,0:T(8,128)(2,1)} fusion(bf16[256,256,128]{2,1,0:T(8,128)(2,1)} %get-tuple-element.148, s32[1024]{0:T(1024)S(1)} %pad_clamp_fusion.4), kind=kCustom, calls=%fused_computation.clone.clone.1 | custom fusion | bytes 4194432 | tf_op jit(solution)/shard_map/while/body/eval_jaxpr/gather | solution.py:84
  329.4 6.1 %fusion.54 = f32[32,256,128]{2,1,0:T(8,128)} fusion(bf16[32,256,128]{2,1,0:T(8,128)(2,1)} %gather_fusion, bf16[5,32,256,256]{3,2,1,0:T(8,128)(2,1)} %get-tuple-element.146, s32[]{:T(128)} %get-tuple-element.135), kind=kOutput, calls=%fused_computation.3.clone.1 | convolution fusion | flops 536870912 | bytes 10486272 | tf_op jit(solution)/shard_map/while/body/eval_jaxpr/tij,tjc->tic/dot_general | solution.py:85
  335.4 7.6 %fusion.55 = f32[2,256,128]{2,0,1:T(2,128)S(1)} fusion(f32[32,256,128]{2,1,0:T(8,128)} %fusion.54, f32[2,256,128]{2,0,1:T(2,128)S(1)} %get-tuple-element.136, pred[]{:T(512)S(6)} %compare.3, f32[5,32,2]{1,2,0:T(2,128)S(1)} %get-tuple-element.145, s32[]{:T(128)} %get-tuple-element.135), kind=kOutput, calls=%fused_computation.8.clone.1 | convolution fusion | flops 25296896 | bytes 4719621 | tf_op jit(solution)/shard_map/while/body/eval_jaxpr/tb,tic->bic/dot_general | solution.py:88
  343.0 7.9 %gather_fusion = bf16[32,256,128]{2,1,0:T(8,128)(2,1)} fusion(bf16[256,256,128]{2,1,0:T(8,128)(2,1)} %get-tuple-element.148, s32[1024]{0:T(1024)S(1)} %pad_clamp_fusion.4), kind=kCustom, calls=%fused_computation.clone.clone.1 | custom fusion | bytes 4194432 | tf_op jit(solution)/shard_map/while/body/eval_jaxpr/gather | solution.py:84
  351.0 6.1 %fusion.54 = f32[32,256,128]{2,1,0:T(8,128)} fusion(bf16[32,256,128]{2,1,0:T(8,128)(2,1)} %gather_fusion, bf16[5,32,256,256]{3,2,1,0:T(8,128)(2,1)} %get-tuple-element.146, s32[]{:T(128)} %get-tuple-element.135), kind=kOutput, calls=%fused_computation.3.clone.1 | convolution fusion | flops 536870912 | bytes 10486272 | tf_op jit(solution)/shard_map/while/body/eval_jaxpr/tij,tjc->tic/dot_general | solution.py:85
  357.0 7.6 %fusion.55 = f32[2,256,128]{2,0,1:T(2,128)S(1)} fusion(f32[32,256,128]{2,1,0:T(8,128)} %fusion.54, f32[2,256,128]{2,0,1:T(2,128)S(1)} %get-tuple-element.136, pred[]{:T(512)S(6)} %compare.3, f32[5,32,2]{1,2,0:T(2,128)S(1)} %get-tuple-element.145, s32[]{:T(128)} %get-tuple-element.135), kind=kOutput, calls=%fused_computation.8.clone.1 | convolution fusion | flops 25296896 | bytes 4719621 | tf_op jit(solution)/shard_map/while/body/eval_jaxpr/tb,tic->bic/dot_general | solution.py:88
  364.6 7.9 %gather_fusion = bf16[32,256,128]{2,1,0:T(8,128)(2,1)} fusion(bf16[256,256,128]{2,1,0:T(8,128)(2,1)} %get-tuple-element.148, s32[1024]{0:T(1024)S(1)} %pad_clamp_fusion.4), kind=kCustom, calls=%fused_computation.clone.clone.1 | custom fusion | bytes 4194432 | tf_op jit(solution)/shard_map/while/body/eval_jaxpr/gather | solution.py:84
  372.6 6.1 %fusion.54 = f32[32,256,128]{2,1,0:T(8,128)} fusion(bf16[32,256,128]{2,1,0:T(8,128)(2,1)} %gather_fusion, bf16[5,32,256,256]{3,2,1,0:T(8,128)(2,1)} %get-tuple-element.146, s32[]{:T(128)} %get-tuple-element.135), kind=kOutput, calls=%fused_computation.3.clone.1 | convolution fusion | flops 536870912 | bytes 10486272 | tf_op jit(solution)/shard_map/while/body/eval_jaxpr/tij,tjc->tic/dot_general | solution.py:85
  378.6 7.6 %fusion.55 = f32[2,256,128]{2,0,1:T(2,128)S(1)} fusion(f32[32,256,128]{2,1,0:T(8,128)} %fusion.54, f32[2,256,128]{2,0,1:T(2,128)S(1)} %get-tuple-element.136, pred[]{:T(512)S(6)} %compare.3, f32[5,32,2]{1,2,0:T(2,128)S(1)} %get-tuple-element.145, s32[]{:T(128)} %get-tuple-element.135), kind=kOutput, calls=%fused_computation.8.clone.1 | convolution fusion | flops 25296896 | bytes 4719621 | tf_op jit(solution)/shard_map/while/body/eval_jaxpr/tb,tic->bic/dot_general | solution.py:88
  386.2 7.9 %gather_fusion = bf16[32,256,128]{2,1,0:T(8,128)(2,1)} fusion(bf16[256,256,128]{2,1,0:T(8,128)(2,1)} %get-tuple-element.148, s32[1024]{0:T(1024)S(1)} %pad_clamp_fusion.4), kind=kCustom, calls=%fused_computation.clone.clone.1 | custom fusion | bytes 4194432 | tf_op jit(solution)/shard_map/while/body/eval_jaxpr/gather | solution.py:84
  394.2 6.1 %fusion.54 = f32[32,256,128]{2,1,0:T(8,128)} fusion(bf16[32,256,128]{2,1,0:T(8,128)(2,1)} %gather_fusion, bf16[5,32,256,256]{3,2,1,0:T(8,128)(2,1)} %get-tuple-element.146, s32[]{:T(128)} %get-tuple-element.135), kind=kOutput, calls=%fused_computation.3.clone.1 | convolution fusion | flops 536870912 | bytes 10486272 | tf_op jit(solution)/shard_map/while/body/eval_jaxpr/tij,tjc->tic/dot_general | solution.py:85
  400.2 7.6 %fusion.55 = f32[2,256,128]{2,0,1:T(2,128)S(1)} fusion(f32[32,256,128]{2,1,0:T(8,128)} %fusion.54, f32[2,256,128]{2,0,1:T(2,128)S(1)} %get-tuple-element.136, pred[]{:T(512)S(6)} %compare.3, f32[5,32,2]{1,2,0:T(2,128)S(1)} %get-tuple-element.145, s32[]{:T(128)} %get-tuple-element.135), kind=kOutput, calls=%fused_computation.8.clone.1 | convolution fusion | flops 25296896 | bytes 4719621 | tf_op jit(solution)/shard_map/while/body/eval_jaxpr/tb,tic->bic/dot_general | solution.py:88
  407.9 1.1 fusion.16
  409.0 0.2 copy-done.1
  (65 shorter events, 0.5 us)
Async XLA Ops:
  0.0 20.0 %copy-start = (bf16[6144,128]{1,0:T(8,128)(2,1)S(1)}, bf16[6144,128]{1,0:T(8,128)(2,1)}, u32[]{:S(2)}) copy-start(bf16[6144,128]{1,0:T(8,128)(2,1)} %param.11) | copy-start | bytes 4718596
  43.6 9.8 %copy-start.4 = (s32[16,32]{1,0:T(8,128)S(1)}, s32[16,32]{1,0:T(8,128)}, u32[]{:S(2)}) copy-start(s32[16,32]{1,0:T(8,128)} %param.18) | copy-start | bytes 6148
  43.6 17.9 %copy-start.5 = (s32[160]{0:T(256)S(1)}, s32[160]{0:T(256)}, u32[]{:S(2)}) copy-start(s32[160]{0:T(256)} %param.14) | copy-start | bytes 1924
  43.6 18.0 %copy-start.2 = (bf16[16,32,128]{2,1,0:T(8,128)(2,1)S(1)}, bf16[16,32,128]{2,1,0:T(8,128)(2,1)}, u32[]{:S(2)}) copy-start(bf16[16,32,128]{2,1,0:T(8,128)(2,1)} %param.17) | copy-start | bytes 393220
  43.6 256.0 %all-to-all-start.1 = ((bf16[128,2,256,128]{3,2,1,0:T(8,128)(2,1)}), bf16[128,2,256,128]{3,2,1,0:T(8,128)(2,1)}, u32[]{:S(2)}, u32[]{:S(2)}) async-start(bf16[128,2,256,128]{3,2,1,0:T(8,128)(2,1)} %broadcast_select_fusion), calls=%async_computation.1 | async-start | bytes 33554432 | tf_op jit(solution)/shard_map/all_to_all | solution.py:70
  53.5 224.7 %collective-permute-start.4 = (bf16[1,32]{1,0:T(2,128)(2,1)S(1)}, bf16[1,32]{1,0:T(2,128)(2,1)S(1)}, u32[]{:S(2)}, u32[]{:S(2)}) collective-permute-start(bf16[1,32]{1,0:T(2,128)(2,1)S(1)} %get-tuple-element.86), channel_id=1, source_target_pairs={{0,1},{1,2},{2,3},{3,4},{4,5},{5,6},{6,7},{7,8},{8,9},{9,10},{10,1... | collective-permute-start | bytes 200 | tf_op jit(solution)/shard_map/ppermute | solution.py:16
  57.0 219.3 %collective-permute-start = (bf16[16,1]{1,0:T(8,128)(2,1)S(1)}, bf16[16,1]{1,0:T(8,128)(2,1)S(1)}, u32[]{:S(2)}, u32[]{:S(2)}) collective-permute-start(bf16[16,1]{1,0:T(8,128)(2,1)S(1)} %get-tuple-element.84), channel_id=1, source_target_pairs={{0,16},{16,32},{32,48},{48,64},{64,80},{80,96},{96,112},{112,0},{1... | collective-permute-start | bytes 104 | tf_op jit(solution)/shard_map/ppermute | solution.py:16
  57.0 219.3 %collective-permute-start.2 = (bf16[16,1]{1,0:T(8,128)(2,1)S(1)}, bf16[16,1]{1,0:T(8,128)(2,1)S(1)}, u32[]{:S(2)}, u32[]{:S(2)}) collective-permute-start(bf16[16,1]{1,0:T(8,128)(2,1)S(1)} %get-tuple-element.85), channel_id=1, source_target_pairs={{16,0},{32,16},{48,32},{64,48},{80,64},{96,80},{112,96},{0,112},{1... | collective-permute-start | bytes 104 | tf_op jit(solution)/shard_map/ppermute | solution.py:17
  58.8 223.3 %collective-permute-start.6 = (bf16[32]{0:T(256)(128)(2,1)S(1)}, bf16[32]{0:T(256)(128)(2,1)S(1)}, u32[]{:S(2)}, u32[]{:S(2)}) collective-permute-start(bf16[32]{0:T(256)(128)(2,1)S(1)} %rev.8), channel_id=1, source_target_pairs={{0,16},{16,0},{32,48},{48,32},{64,80},{80,64},{96,112},{112,96},{1... | collective-permute-start | bytes 200 | tf_op jit(solution)/shard_map/ppermute | solution.py:25
  58.9 226.9 %collective-permute-start.9 = (bf16[1,32]{1,0:T(2,128)(2,1)S(1)}, bf16[1,32]{1,0:T(2,128)(2,1)S(1)}, u32[]{:S(2)}, u32[]{:S(2)}) collective-permute-start(bf16[1,32]{1,0:T(2,128)(2,1)S(1)} %get-tuple-element.87), channel_id=1, source_target_pairs={{1,0},{2,1},{3,2},{4,3},{5,4},{6,5},{7,6},{8,7},{9,8},{10,9},{11,1... | collective-permute-start | bytes 200 | tf_op jit(solution)/shard_map/ppermute | solution.py:17
  276.2 14.6 %collective-permute-start.10 = (bf16[32,128]{1,0:T(8,128)(2,1)S(1)}, bf16[32,128]{1,0:T(8,128)(2,1)S(1)}, u32[]{:S(2)}, u32[]{:S(2)}) collective-permute-start(bf16[32,128]{1,0:T(8,128)(2,1)S(1)} %rev.9), channel_id=1, source_target_pairs={{0,16},{16,0},{32,48},{48,32},{64,80},{80,64},{96,112},{112,96},{1... | collective-permute-start | bytes 24584 | tf_op jit(solution)/shard_map/ppermute | solution.py:25
  276.3 18.5 %collective-permute-start.13 = (bf16[1,32,128]{2,1,0:T(8,128)(2,1)S(1)}, bf16[1,32,128]{2,1,0:T(8,128)(2,1)S(1)}, u32[]{:S(2)}, u32[]{:S(2)}) collective-permute-start(bf16[1,32,128]{2,1,0:T(8,128)(2,1)S(1)} %get-tuple-element.76), channel_id=1, source_target_pairs={{1,0},{2,1},{3,2},{4,3},{5,4},{6,5},{7,6},{8,7},{9,8},{10,9},{11,1... | collective-permute-start | bytes 24584 | tf_op jit(solution)/shard_map/ppermute | solution.py:17
  278.2 129.7 %collective-permute-start.5 = (bf16[1,32,128]{2,1,0:T(8,128)(2,1)S(1)}, bf16[1,32,128]{2,1,0:T(8,128)(2,1)S(1)}, u32[]{:S(2)}, u32[]{:S(2)}) collective-permute-start(bf16[1,32,128]{2,1,0:T(8,128)(2,1)S(1)} %get-tuple-element.78), channel_id=1, source_target_pairs={{0,1},{1,2},{2,3},{3,4},{4,5},{5,6},{6,7},{7,8},{8,9},{9,10},{10,1... | collective-permute-start | bytes 24584 | tf_op jit(solution)/shard_map/ppermute | solution.py:16
  282.1 3.6 collective-permute-start.7
  285.8 5.1 %collective-permute-start.8 = (bf16[32]{0:T(256)(128)(2,1)S(1)}, bf16[32]{0:T(256)(128)(2,1)S(1)}, u32[]{:S(2)}, u32[]{:S(2)}) collective-permute-start(bf16[32]{0:T(256)(128)(2,1)S(1)} %collective-permute-done.7), channel_id=1, source_target_pairs={{0,64},{16,80},{32,96},{48,112},{64,0},{80,16},{96,32},{112,48},{1... | collective-permute-start | bytes 200 | tf_op jit(solution)/shard_map/ppermute | solution.py:25
  285.8 122.1 %collective-permute-start.1 = (bf16[16,1,128]{2,1,0:T(2,128)(2,1)S(1)}, bf16[16,1,128]{2,1,0:T(2,128)(2,1)S(1)}, u32[]{:S(2)}, u32[]{:S(2)}) collective-permute-start(bf16[16,1,128]{2,1,0:T(2,128)(2,1)S(1)} %get-tuple-element.79), channel_id=1, source_target_pairs={{0,16},{16,32},{32,48},{48,64},{64,80},{80,96},{96,112},{112,0},{1... | collective-permute-start | bytes 12296 | tf_op jit(solution)/shard_map/ppermute | solution.py:16
  290.8 117.0 %collective-permute-start.3 = (bf16[16,1,128]{2,1,0:T(2,128)(2,1)S(1)}, bf16[16,1,128]{2,1,0:T(2,128)(2,1)S(1)}, u32[]{:S(2)}, u32[]{:S(2)}) collective-permute-start(bf16[16,1,128]{2,1,0:T(2,128)(2,1)S(1)} %get-tuple-element.80), channel_id=1, source_target_pairs={{16,0},{32,16},{48,32},{64,48},{80,64},{96,80},{112,96},{0,112},{1... | collective-permute-start | bytes 12296 | tf_op jit(solution)/shard_map/ppermute | solution.py:17
  290.9 3.7 collective-permute-start.11
  294.5 5.2 %collective-permute-start.12 = (bf16[32,128]{1,0:T(8,128)(2,1)S(1)}, bf16[32,128]{1,0:T(8,128)(2,1)S(1)}, u32[]{:S(2)}, u32[]{:S(2)}) collective-permute-start(bf16[32,128]{1,0:T(8,128)(2,1)S(1)} %collective-permute-done.11), channel_id=1, source_target_pairs={{0,64},{16,80},{32,96},{48,112},{64,0},{80,16},{96,32},{112,48},{1... | collective-permute-start | bytes 24584 | tf_op jit(solution)/shard_map/ppermute | solution.py:25
  299.7 108.2 %copy-start.3 = (bf16[16,32,128]{2,1,0:T(8,128)(2,1)S(1)}, bf16[16,32,128]{2,1,0:T(8,128)(2,1)}, u32[]{:S(2)}) copy-start(bf16[16,32,128]{2,1,0:T(8,128)(2,1)} %param.17) | copy-start | bytes 393220
  299.7 108.2 %slice-start = ((bf16[16,32,128]{2,1,0:T(8,128)(2,1)}), bf16[15,32,128]{2,1,0:T(8,128)(2,1)S(1)}, s32[]{:S(2)}) async-start(bf16[16,32,128]{2,1,0:T(8,128)(2,1)} %param.17), calls=%async_computation.2 | async-start | bytes 245760 | tf_op jit(solution)/shard_map/slice | solution.py:119
  299.7 108.2 %copy-start.6 = (f32[128]{0:T(128)S(1)}, f32[128]{0:T(128)}, u32[]{:S(2)}) copy-start(f32[128]{0:T(128)} %param.19) | copy-start | bytes 1540
  407.8 1.4 copy-start.1
where the time goes:
time: 410 us; the launch traced here: 409 us
  waiting for transfers between devices  232 us (57%)
  matrix products  68.1 us (17%)
  local copies, waits for them, and re-layouts  52.7 us (13%)
  starting transfers between devices  23.5 us (6%)
  other arithmetic  16.5 us (4%)
  blocking collectives  15.6 us (4%)
    ppermute x4, waiting for transfers between devices, padded(): before = lax.ppermute(last, axis, up)  215 us
    gather x5, local copies, waits for them, and re-layouts, advance(): gathered = arrived[group_slots]  39.8 us
    dot_general x5, matrix products, advance(): jnp.einsum('tb,tic->bic', group_select, partial_sum, precision=lax.Precis...  37.8 us
    dot_general x5, matrix products, advance(): jnp.einsum('tij,tjc->tic', weights, gathered, preferred_element_type=jnp....  30.3 us
    ppermute x6, waiting for transfers between devices, partner(): return lax.ppermute(value, axis, pairs)  17.1 us
    all_to_all x1, blocking collectives, local(): lax.all_to_all(asking.reshape(devices, per_peer), ('gx', 'gy'), split_axi...  15.6 us
    select_n x1, other arithmetic, local(): jnp.where((wanted > 0)[:, None, None], block_table[jnp.maximum(wanted - 1...  14 us
    all_to_all x1, starting transfers between devices, local(): lax.all_to_all(outgoing, ('gx', 'gy'), split_axis=0, concat_axis=0, tiled...  9.8 us
  transfers between devices with their start and end apart: 15, of which 5 were waited for; matrix products, arithmetic and copies ran while one was open for 27% of the time, Pallas kernels for 0%

commit v1 on v0

v1 whole, which is shorter than its diff:
```python
import functools

import jax
import jax.numpy as jnp
from jax import lax
from jax.experimental import pallas as pl
from jax.experimental.pallas import tpu as pltpu
from jax.sharding import PartitionSpec as P

MESH = pl.DeviceIdType.MESH
ROWS = 256
CHANNELS = 128
BLOCKS = 24
RING = 4
CORES = 2
CLASSES = ((0, 96, "xyz"), (96, 80, "yzx"), (176, 80, "zxy"))
FAR = (1, 3, 2)
GROUP = 8
DEPTH = 4


def digit(axis, value):
    return {"x": value // 32, "z": value // 4 % 4, "y": value % 4}[axis]


def peer(axis, offset, flip=0):
    gx, gy = lax.axis_index("gx"), lax.axis_index("gy")
    x, core, z, y = gx // 2, gx % 2, gy // 4, gy % 4
    if axis == "x":
        x = (x + offset) % RING
    if axis == "y":
        y = (y + offset) % RING
    if axis == "z":
        z = (z + offset) % RING
    core = (core + flip) % CORES
    return (x * 2 + core, z * 4 + y)


def slot_of(distance, core, rank):
    return (
        ((distance["x"] * CORES + core) * RING + distance["z"]) * RING + distance["y"]
    ) * 2 + rank


def exchange_kernel(ask, atm, final, *scratch):
    gathered, sent, relayed, first, second = (scratch[3 * i : 3 * i + 3] for i in range(5))
    table, ask_sem, ask_s, ask_r, mid_s, mid_r, smem_sem, own_sem, ag_s, ag_r, p2_s, p2_r, p3_s, p3_r = scratch[15:]

    barrier = pltpu.get_barrier_semaphore()
    neighbours = [(a, o, f) for a in "xyz" for o in (1, 2, 3) for f in (0, 1)] + [("x", 0, 1)]
    for axis, offset, flip in neighbours:
        pl.semaphore_signal(barrier, 1, device_id=peer(axis, offset, flip), device_id_type=MESH)
    pl.semaphore_wait(barrier, len(neighbours))

    def remote(src, dst, send, recv, target):
        copy = pltpu.make_async_remote_copy(
            src_ref=src, dst_ref=dst, send_sem=send, recv_sem=recv, device_id=target, device_id_type=MESH
        )
        copy.start()
        return copy

    asks, mids, owns, rings, p2s, p3s = [], [], [], [], [], []
    for c, (_, _, order) in enumerate(CLASSES):
        local = pltpu.make_async_copy(ask, first[c].at[0], ask_sem.at[c])
        local.start()
        asks.append([local])
        for lane in range(1, RING * CORES):
            o3, flip = lane // CORES, lane % CORES
            asks[c].append(
                remote(ask, first[c].at[lane], ask_s.at[c, lane], ask_r.at[c, lane], peer(order[2], -o3, flip))
            )
    for c, (start, size, order) in enumerate(CLASSES):
        block = atm.at[:, pl.ds(start, size)]
        rings.append(
            [remote(block, gathered[c].at[o], ag_s.at[c, o], ag_r.at[c, o], peer(order[0], o)) for o in FAR]
        )
        own = pltpu.make_async_copy(block, gathered[c].at[0], own_sem.at[c])
        own.start()
        owns.append(own)
    for c, (_, _, order) in enumerate(CLASSES):
        for copy in asks[c]:
            copy.wait()
        mids.append(
            [remote(first[c], second[c].at[o], mid_s.at[c, o], mid_r.at[c, o], peer(order[1], -o)) for o in FAR]
        )
        keep = pltpu.make_async_copy(first[c], table.at[c, 0], smem_sem.at[c, 0])
        keep.start()
        mids[c].append(keep)
    for c in range(3):
        for copy in mids[c]:
            copy.wait()
        keeps = []
        for o in FAR:
            keep = pltpu.make_async_copy(second[c].at[o], table.at[c, o], smem_sem.at[c, o])
            keep.start()
            keeps.append(keep)
        for keep in keeps:
            keep.wait()
    for c in range(3):
        owns[c].wait()
        for copy in rings[c]:
            copy.wait()

    def pack(c, o2):
        order = CLASSES[c][2]

        def body(lane, carry):
            o3, flip = lane // CORES, lane % CORES
            for o1 in range(RING):
                for rank in range(2):
                    at = slot_of({order[0]: o1, order[1]: o2, order[2]: o3}, flip, rank)
                    which = table[c, o2, lane, at // 128, at % 128]
                    sent[c][o2, lane, o1, rank] = gathered[c][o1, which]
            return carry

        lax.fori_loop(0, RING * CORES, body, 0)

    def send2(c, o2):
        order = CLASSES[c][2]
        return remote(
            sent[c].at[o2], relayed[c].at[o2], p2_s.at[c, o2], p2_r.at[c, o2], peer(order[1], o2)
        )

    def send3(c, o2):
        start, size, order = CLASSES[c]
        source = sent[c] if o2 == 0 else relayed[c]
        for lane in range(RING * CORES):
            o3, flip = lane // CORES, lane % CORES
            at = {order[0]: slice(None), order[1]: o2, order[2]: o3}
            dst = final.at[at["x"], flip, at["z"], at["y"], :, pl.ds(start, size)]
            src = source.at[o2, lane]
            if lane == 0:
                copy = pltpu.make_async_copy(src, dst, p3_s.at[c, o2, 0])
                copy.start()
                p3s.append(copy)
            else:
                p3s.append(
                    remote(src, dst, p3_s.at[c, o2, lane], p3_r.at[c, o2, lane], peer(order[2], o3, flip))
                )

    steps = [(c, o2) for o2 in FAR + (0,) for c in range(3)]
    pending = {}
    for i, (c, o2) in enumerate(steps + [None]) if False else enumerate(steps):
        pack(c, o2)
        if i > 0:
            cc, oo = steps[i - 1]
            if oo:
                pending[cc, oo] = send2(cc, oo)
            else:
                send3(cc, oo)
    send3(*steps[-1])
    for o2 in FAR:
        for c in range(3):
            pending[c, o2].wait()
            send3(c, o2)
    for copy in p3s:
        copy.wait()


def exchange(ask, atm):
    dma = pltpu.SemaphoreType.DMA
    tables = RING * CORES
    scratch = [pltpu.VMEM((RING, BLOCKS, size, CHANNELS), jnp.bfloat16) for _, size, _ in CLASSES]
    for _ in range(2):
        scratch += [
            pltpu.VMEM((RING, tables, RING, 2, size, CHANNELS), jnp.bfloat16) for _, size, _ in CLASSES
        ]
    scratch += [pltpu.VMEM((tables, 2, 128), jnp.int32) for _ in CLASSES]
    scratch += [pltpu.VMEM((RING, tables, 2, 128), jnp.int32) for _ in CLASSES]
    scratch += [
        pltpu.SMEM((3, RING, tables, 2, 128), jnp.int32),
        dma((3,)),
        dma((3, tables)),
        dma((3, tables)),
        dma((3, RING)),
        dma((3, RING)),
        dma((3, RING)),
        dma((3,)),
        dma((3, RING)),
        dma((3, RING)),
        dma((3, RING)),
        dma((3, RING)),
        dma((3, RING, tables)),
        dma((3, RING, tables)),
    ]
    return pl.pallas_call(
        exchange_kernel,
        out_shape=jax.ShapeDtypeStruct((RING, CORES, RING, RING, 2, ROWS, CHANNELS), jnp.bfloat16),
        in_specs=[pl.BlockSpec(memory_space=pltpu.VMEM), pl.BlockSpec(memory_space=pl.ANY)],
        out_specs=pl.BlockSpec(memory_space=pl.ANY),
        scratch_shapes=scratch,
        compiler_params=pltpu.CompilerParams(
            collective_id=0, has_side_effects=True, vmem_limit_bytes=56 * 2**20
        ),
        name="exchange",
    )(ask, atm)


def remap_kernel(count, slots, targets, weight, blocks, out, w_buf, x_buf, w_sem, x_sem):
    live = count[0]
    steps = (live + GROUP - 1) // GROUP

    def copies(step, at):
        first = step * GROUP
        yield pltpu.make_async_copy(weight.at[pl.ds(first, GROUP)], w_buf.at[at], w_sem.at[at])
        for i in range(GROUP):
            yield pltpu.make_async_copy(blocks.at[slots[first + i]], x_buf.at[at, i], x_sem.at[at, i])

    def fetch(step):
        @pl.when(step < steps)
        def _():
            for copy in copies(step, lax.rem(step, DEPTH)):
                copy.start()

    out[...] = jnp.zeros_like(out)
    for step in range(DEPTH - 1):
        fetch(step)

    def body(step, carry):
        at = lax.rem(step, DEPTH)
        fetch(step + DEPTH - 1)
        for copy in copies(step, at):
            copy.wait()
        for i in range(GROUP):
            tile = step * GROUP + i

            @pl.when(tile < live)
            def _():
                out[targets[tile]] += jnp.dot(
                    w_buf[at, i], x_buf[at, i], preferred_element_type=jnp.float32
                )

        return carry

    lax.fori_loop(0, steps, body, 0)


def remap(count, slots, targets, weight, blocks):
    smem = pl.BlockSpec(memory_space=pltpu.SMEM)
    hbm = pl.BlockSpec(memory_space=pl.ANY)
    dma = pltpu.SemaphoreType.DMA
    return pl.pallas_call(
        remap_kernel,
        out_shape=jax.ShapeDtypeStruct((2, ROWS, CHANNELS), jnp.float32),
        in_specs=[smem, smem, smem, hbm, hbm],
        out_specs=pl.BlockSpec(memory_space=pltpu.VMEM),
        scratch_shapes=[
            pltpu.VMEM((DEPTH, GROUP, ROWS, ROWS), jnp.bfloat16),
            pltpu.VMEM((DEPTH, GROUP, ROWS, CHANNELS), jnp.bfloat16),
            dma((DEPTH,)),
            dma((DEPTH, GROUP)),
        ],
        compiler_params=pltpu.CompilerParams(vmem_limit_bytes=24 * 2**20),
        name="remap",
    )(count, slots, targets, weight, blocks)


def plan(tile_src, atm_pos):
    positions = atm_pos[tile_src]
    owners = positions // BLOCKS
    ordinal = jnp.arange(tile_src.shape[0], dtype=jnp.int32)
    earlier = (owners[:, None] == owners[None, :]) & (ordinal[None, :] < ordinal[:, None])
    rank = jnp.sum(earlier.astype(jnp.int32), axis=1)
    gx, gy = lax.axis_index("gx"), lax.axis_index("gy")
    ox, oy = owners // 16, owners % 16
    distance = {
        "x": (gx // 2 - ox // 2) % RING,
        "z": (gy // 4 - oy // 4) % RING,
        "y": (gy % 4 - oy % 4) % RING,
    }
    slots = slot_of(distance, (gx - ox) % CORES, rank)
    matches = slots[None, :] == jnp.arange(256, dtype=jnp.int32)[:, None]
    ask = jnp.sum(jnp.where(matches, (positions % BLOCKS)[None, :], 0), axis=1)
    return slots, ask.reshape(2, 128)


def with_mask(state, mask):
    wide = jnp.broadcast_to(mask[..., None], state.shape)
    return jnp.concatenate([state, wide], axis=0)


def local(atm_fields, atm_pos, tile_src, tile_tgt, tile_count, tile_weight, ocean_state, land_mask, mixing):
    n_gx, n_gy = lax.axis_size("gx"), lax.axis_size("gy")
    mask_half = land_mask.astype(jnp.bfloat16)
    lat, lon = mask_half.shape
    ring_up = [(i, (i + 1) % n_gx) for i in range(n_gx)]
    ring_down = [(j, i) for i, j in ring_up]
    line_up = [(i, i + 1) for i in range(n_gy - 1)]
    line_down = [(j, i) for i, j in line_up]
    west = lax.ppermute(with_mask(ocean_state[:, -1], mask_half[:, -1]), "gx", ring_up)
    east = lax.ppermute(with_mask(ocean_state[:, 0], mask_half[:, 0]), "gx", ring_down)
    top = with_mask(ocean_state[-1], mask_half[-1])
    south = lax.ppermute(top, "gy", line_up)
    north = lax.ppermute(with_mask(ocean_state[0], mask_half[0]), "gy", line_down)
    flipped = with_mask(ocean_state[-1, ::-1], mask_half[-1, ::-1])
    fold = lax.ppermute(flipped, "gx", [(i, n_gx - 1 - i) for i in range(n_gx)])

    slots, ask = plan(tile_src, atm_pos)
    blocks = exchange(ask, atm_fields.reshape(BLOCKS, ROWS, CHANNELS))
    remapped = remap(tile_count, slots, tile_tgt, tile_weight, blocks.reshape(256, ROWS, CHANNELS))
    forcing = remapped.reshape(lat, lon, CHANNELS)

    north = jnp.where(lax.axis_index("gy") == n_gy - 1, fold, north)
    center = ocean_state.astype(jnp.float32)
    wet = jnp.broadcast_to(mask_half[..., None], ocean_state.shape)

    def around(values, part):
        lead, tail = (lambda v, n: v[:n], lambda v, n: v[n:])
        pick = lead if part == 0 else tail
        w, e = pick(west, lat)[:, None], pick(east, lat)[:, None]
        s, n = pick(south, lon)[None], pick(north, lon)[None]
        return (
            jnp.concatenate([w, values[:, :-1]], axis=1),
            jnp.concatenate([values[:, 1:], e], axis=1),
            jnp.concatenate([s, values[:-1]], axis=0),
            jnp.concatenate([values[1:], n], axis=0),
        )

    diffusion = jnp.zeros_like(center)
    for side_state, side_mask in zip(around(ocean_state, 0), around(wet, 1)):
        diffusion = diffusion + side_mask.astype(jnp.float32) * (side_state.astype(jnp.float32) - center)
    result = wet.astype(jnp.float32) * (center + forcing + mixing * diffusion)
    return result.astype(jnp.bfloat16)


def solution(mesh):
    both = ("gx", "gy")
    in_specs = (
        P(both, None),
        P(),
        P(both),
        P(both),
        P(both),
        P(both, None, None),
        P("gy", "gx", None),
        P("gy", "gx"),
        P(),
    )
    return jax.shard_map(
        local, mesh=mesh, in_specs=in_specs, out_specs=P("gy", "gx", None), check_vma=False
    )
```

time: 410 us -> 238 us (0.58)
  the two profiles are of different devices: /device:TPU:74 before, /device:TPU:1 now
where the time goes in v1:
time: 238 us; the launch traced here: 236 us
  Pallas kernels  209 us (88%)
  local copies, waits for them, and re-layouts  12.1 us (5%)
  starting transfers between devices  9.65 us (4%)
  other arithmetic  3.71 us (2%)
    pallas_call x1, Pallas kernels, exchange(): pl.pallas_call(exchange_kernel, out_shape=jax.ShapeDtypeStruct((RING, COR...  169 us
    pallas_call x1, Pallas kernels, remap(): pl.pallas_call(remap_kernel, out_shape=jax.ShapeDtypeStruct((2, ROWS, CHA...  40.5 us
    unnamed x12, local copies, waits for them, and re-layouts  5.78 us
  transfers between devices with their start and end apart: 5, of which 0 were waited for; matrix products, arithmetic and copies ran while one was open for 3% of the time, Pallas kernels for 89%

profile of v1, /device:TPU:1, one launch (start us, length us, event | category | flops | bytes accessed | tf_op | source)
XLA Modules:
  0.0 235.8 jit_solution(10333902354993768733)
XLA Ops:
  0.0 0.0 copy-start
  0.0 0.0 copy-start.2
  0.0 0.7 fusion.21
  0.7 0.1 rev.7
  0.8 0.7 slice_bitcast_fusion.4
  1.6 0.1 pad.7.clone
  1.7 0.1 pad_maximum_fusion.1
  1.7 3.9 %collective-permute-start.3 = (bf16[64,128]{1,0:T(8,128)(2,1)S(1)}, bf16[64,128]{1,0:T(8,128)(2,1)S(1)}, u32[]{:S(2)}, u32[]{:S(2)}) collective-permute-start(bf16[64,128]{1,0:T(8,128)(2,1)S(1)} %pad_maximum_fusion.1), channel_id=1, source_target_pairs={{0,112},{16,96},{32,80},{48,64},{64,48},{80,32},{96,16},{112,0},{1... | collective-permute-start | bytes 49160 | tf_op jit(solution)/shard_map/ppermute | solution.py:296
  5.6 0.1 pad.5.clone
  5.7 0.1 pad_maximum_fusion.2
  5.8 1.3 collective-permute-start.4
  7.1 0.1 pad.13.clone
  7.1 0.1 pad_maximum_fusion
  7.2 4.0 %collective-permute-start.2 = (bf16[64,128]{1,0:T(8,128)(2,1)S(1)}, bf16[64,128]{1,0:T(8,128)(2,1)S(1)}, u32[]{:S(2)}, u32[]{:S(2)}) collective-permute-start(bf16[64,128]{1,0:T(8,128)(2,1)S(1)} %pad_maximum_fusion), channel_id=1, source_target_pairs={{0,1},{1,2},{2,3},{3,4},{4,5},{5,6},{6,7},{7,8},{8,9},{9,10},{10,1... | collective-permute-start | bytes 49160 | tf_op jit(solution)/shard_map/ppermute | solution.py:293
  11.2 0.2 slice_reduce_fusion
  11.4 0.8 fusion.24
  12.2 0.1 pad.25.clone
  12.3 0.1 pad_maximum_fusion.3
  12.3 0.2 collective-permute-start
  12.6 0.1 pad.19.clone
  12.6 0.1 pad_maximum_fusion.4
  12.7 0.3 collective-permute-start.1
  13.0 0.1 fusion.26
  13.1 1.0 fusion.23
  14.1 1.0 fusion.22
  15.1 0.7 compare_select_fusion
  15.8 0.0 copy-done
  15.8 1.4 gather_fusion
  17.3 0.2 convert_reduce_fusion
  17.5 0.7 select_reduce_fusion
  18.9 168.9 %exchange.1 = bf16[4,2,4,4,2,256,128]{6,5,4,3,2,1,0:T(8,128)(2,1)} custom-call(s32[2,128]{1,0:T(2,128)} %bitcast.42, bf16[24,256,128]{2,1,0:T(8,128)(2,1)} %bitcast.38), custom_call_target="tpu_custom_call" | custom-call | tf_op jit(solution)/shard_map/exchange/pallas_call | solution.py:186
  187.8 0.0 copy-done.2
  187.8 0.0 copy-start.1
  187.8 5.8 %copy-done.1 = bf16[4,2,4,4,2,256,128]{6,5,4,3,2,1,0:T(8,128)(2,1)S(1)} copy-done((bf16[4,2,4,4,2,256,128]{6,5,4,3,2,1,0:T(8,128)(2,1)S(1)}, bf16[4,2,4,4,2,256,128]{6,5,4,3,2,1,0:T(8,128)(2,1)}, u32[]{:S(2)}) %copy-start.1) | copy-done | bytes 16777240
  193.6 0.0 copy-start.3
  193.6 40.5 %remap.1 = f32[2,256,128]{2,1,0:T(8,128)S(1)} custom-call(s32[1]{0:T(128)S(6)} %copy.32.count, s32[160]{0:T(256)S(1)} %multiply_add_fusion.slots, s32[160]{0:T(256)S(1)} %copy-done.2, bf16[160,256,256]{2,1,0:T(8,128)(2,1)} %weight.1, bf16[256,256,128]{2,1,0:T(8,128)(2,1)S(1)} %bitcast.36), custom_call_target="tpu_custom_call" | custom-call | tf_op jit(solution)/shard_map/remap/pallas_call | solution.py:242
  234.1 0.0 collective-permute-done
  234.1 0.0 collective-permute-done.1
  234.2 0.0 collective-permute-done.3
  234.2 0.0 collective-permute-done.4
  234.2 0.0 collective-permute-done.2
  234.3 0.1 broadcast_in_dim.103
  234.4 0.1 broadcast_in_dim.105
  234.5 0.1 broadcast_in_dim.113
  234.7 0.1 broadcast_in_dim.115
  234.8 0.0 copy-done.3
  234.8 0.0 copy-done.4
  234.8 1.0 fusion.2
  (18 shorter events, 0.2 us)
Async XLA Ops:
  0.0 15.8 %copy-start = (s32[3072]{0:T(1024)S(1)}, s32[3072]{0:T(1024)}, u32[]{:S(2)}) copy-start(s32[3072]{0:T(1024)} %param.10) | copy-start | bytes 36868
  0.0 187.8 %copy-start.2 = (s32[160]{0:T(256)S(1)}, s32[160]{0:T(256)}, u32[]{:S(2)}) copy-start(s32[160]{0:T(256)} %targets.1) | copy-start | bytes 1924
  1.7 232.4 %collective-permute-start.3 = (bf16[64,128]{1,0:T(8,128)(2,1)S(1)}, bf16[64,128]{1,0:T(8,128)(2,1)S(1)}, u32[]{:S(2)}, u32[]{:S(2)}) collective-permute-start(bf16[64,128]{1,0:T(8,128)(2,1)S(1)} %pad_maximum_fusion.1), channel_id=1, source_target_pairs={{0,112},{16,96},{32,80},{48,64},{64,48},{80,32},{96,16},{112,0},{1... | collective-permute-start | bytes 49160 | tf_op jit(solution)/shard_map/ppermute | solution.py:296
  5.8 228.4 %collective-permute-start.4 = (bf16[64,128]{1,0:T(8,128)(2,1)S(1)}, bf16[64,128]{1,0:T(8,128)(2,1)S(1)}, u32[]{:S(2)}, u32[]{:S(2)}) collective-permute-start(bf16[64,128]{1,0:T(8,128)(2,1)S(1)} %pad_maximum_fusion.2), channel_id=1, source_target_pairs={{1,0},{2,1},{3,2},{4,3},{5,4},{6,5},{7,6},{8,7},{9,8},{10,9},{11,1... | collective-permute-start | bytes 49160 | tf_op jit(solution)/shard_map/ppermute | solution.py:294
  7.2 227.0 %collective-permute-start.2 = (bf16[64,128]{1,0:T(8,128)(2,1)S(1)}, bf16[64,128]{1,0:T(8,128)(2,1)S(1)}, u32[]{:S(2)}, u32[]{:S(2)}) collective-permute-start(bf16[64,128]{1,0:T(8,128)(2,1)S(1)} %pad_maximum_fusion), channel_id=1, source_target_pairs={{0,1},{1,2},{2,3},{3,4},{4,5},{5,6},{6,7},{7,8},{8,9},{9,10},{10,1... | collective-permute-start | bytes 49160 | tf_op jit(solution)/shard_map/ppermute | solution.py:293
  12.3 221.7 %collective-permute-start = (bf16[32,128]{1,0:T(8,128)(2,1)S(1)}, bf16[32,128]{1,0:T(8,128)(2,1)S(1)}, u32[]{:S(2)}, u32[]{:S(2)}) collective-permute-start(bf16[32,128]{1,0:T(8,128)(2,1)S(1)} %pad_maximum_fusion.3), channel_id=1, source_target_pairs={{0,16},{16,32},{32,48},{48,64},{64,80},{80,96},{96,112},{112,0},{1... | collective-permute-start | bytes 24584 | tf_op jit(solution)/shard_map/ppermute | solution.py:290
  12.7 221.4 %collective-permute-start.1 = (bf16[32,128]{1,0:T(8,128)(2,1)S(1)}, bf16[32,128]{1,0:T(8,128)(2,1)S(1)}, u32[]{:S(2)}, u32[]{:S(2)}) collective-permute-start(bf16[32,128]{1,0:T(8,128)(2,1)S(1)} %pad_maximum_fusion.4), channel_id=1, source_target_pairs={{16,0},{32,16},{48,32},{64,48},{80,64},{96,80},{112,96},{0,112},{1... | collective-permute-start | bytes 24584 | tf_op jit(solution)/shard_map/ppermute | solution.py:291
  187.8 5.8 %copy-start.1 = (bf16[4,2,4,4,2,256,128]{6,5,4,3,2,1,0:T(8,128)(2,1)S(1)}, bf16[4,2,4,4,2,256,128]{6,5,4,3,2,1,0:T(8,128)(2,1)}, u32[]{:S(2)}) copy-start(bf16[4,2,4,4,2,256,128]{6,5,4,3,2,1,0:T(8,128)(2,1)} %exchange.1) | copy-start | bytes 50331652
  193.6 41.2 %copy-start.3 = (bf16[16,32,128]{2,1,0:T(8,128)(2,1)S(1)}, bf16[16,32,128]{2,1,0:T(8,128)(2,1)}, u32[]{:S(2)}) copy-start(bf16[16,32,128]{2,1,0:T(8,128)(2,1)} %param.15) | copy-start | bytes 393220
  193.6 41.2 %copy-start.4 = (f32[128]{0:T(128)S(1)}, f32[128]{0:T(128)}, u32[]{:S(2)}) copy-start(f32[128]{0:T(128)} %param.17) | copy-start | bytes 1540

commit v2 on v1

v2 whole, which is shorter than its diff:
```python
import functools

import jax
import jax.numpy as jnp
from jax import lax
from jax.experimental import pallas as pl
from jax.experimental.pallas import tpu as pltpu
from jax.sharding import PartitionSpec as P

MESH = pl.DeviceIdType.MESH
ROWS = 256
CHANNELS = 128
BLOCKS = 24
RING = 4
CORES = 2
CLASSES = ((0, 96, "xyz"), (96, 80, "yzx"), (176, 80, "zxy"))
FAR = (1, 3, 2)
GROUP = 8
DEPTH = 4
EXCHANGE_VMEM = 56 * 2**20


def peer(axis, offset, flip=0):
    gx, gy = lax.axis_index("gx"), lax.axis_index("gy")
    x, core, z, y = gx // 2, gx % 2, gy // 4, gy % 4
    if axis == "x":
        x = (x + offset) % RING
    if axis == "y":
        y = (y + offset) % RING
    if axis == "z":
        z = (z + offset) % RING
    core = (core + flip) % CORES
    return (x * 2 + core, z * 4 + y)


def where_from(position):
    gx, gy = lax.axis_index("gx"), lax.axis_index("gy")
    owner = lax.shift_right_logical(position * 2731, 16)
    ox, oy = lax.shift_right_logical(owner, 4), owner & 15
    dx = (gx // 2 - lax.shift_right_logical(ox, 1)) & 3
    dk = (gx - ox) & 1
    dz = (gy // 4 - lax.shift_right_logical(oy, 2)) & 3
    dy = (gy - oy) & 3
    return relative({"x": dx, "z": dz, "y": dy}, dk), position - owner * BLOCKS


def relative(distance, core):
    return ((distance["x"] * CORES + core) * RING + distance["z"]) * RING + distance["y"]


def exchange_kernel(positions, sources, atm, state, mask, final, west, east, south, north, masks, firsts, *scratch):
    kept, gathered, sent, relayed, first, second = (scratch[3 * i : 3 * i + 3] for i in range(6))
    (ask, table, ask_sem, ask_s, ask_r, mid_s, mid_r, smem_sem, own_sem, ag_s, ag_r,
     p2_s, p2_r, p3_s, p3_r, edge_s, edge_r) = scratch[18:]

    barrier = pltpu.get_barrier_semaphore()
    neighbours = [(a, o, f) for a in "xyz" for o in (1, 2, 3) for f in (0, 1)] + [("x", 0, 1)]
    for axis, offset, flip in neighbours:
        pl.semaphore_signal(barrier, 1, device_id=peer(axis, offset, flip), device_id_type=MESH)
    gx, gy = lax.axis_index("gx"), lax.axis_index("gy")
    n_gx, n_gy = lax.axis_size("gx"), lax.axis_size("gy")
    is_top = gy == n_gy - 1
    before, after = ((gx + n_gx - 1) % n_gx, gy), ((gx + 1) % n_gx, gy)
    above = (jnp.where(is_top, n_gx - 1 - gx, gx), jnp.where(is_top, gy, gy + 1))
    below = (gx, gy - 1)
    has_below = gy > 0
    for target in (before, after, above):
        pl.semaphore_signal(barrier, 1, device_id=target, device_id_type=MESH)

    @pl.when(has_below)
    def _():
        pl.semaphore_signal(barrier, 1, device_id=below, device_id_type=MESH)

    lane_of = lax.broadcasted_iota(jnp.int32, (1, 128), 1)
    zero = jnp.zeros((1, 128), jnp.int32)

    def claim(step, carry):
        count, ask0, ask1, leader = carry
        for i in range(8):
            tile = step * 8 + i
            lane, block = where_from(positions[sources[tile]])
            mine = lane_of == lane
            free = mine & (count == 0)
            ask0 = jnp.where(free, block, ask0)
            leader = jnp.where(free, tile, leader)
            ask1 = jnp.where(mine, jnp.where(free, ask1, block), ask1)
            count = jnp.where(mine, 1, count)
        return count, ask0, ask1, leader

    _, ask0, ask1, leader = lax.fori_loop(0, sources.shape[0] // 8, claim, (zero, zero, zero, zero))
    ask[0:1] = ask0
    ask[1:2] = ask1
    firsts[...] = leader

    pl.semaphore_wait(barrier, len(neighbours) + 3 + jnp.where(has_below, 1, 0))

    def copier(src, dst, send, recv, target):
        return pltpu.make_async_remote_copy(
            src_ref=src, dst_ref=dst, send_sem=send, recv_sem=recv, device_id=target, device_id_type=MESH
        )

    def remote(*parts):
        copy = copier(*parts)
        copy.start()
        return copy

    half = BLOCKS // 2
    low, high = pl.ds(0, half), pl.ds(half, half)

    def direct(c, i, offset, part):
        start, size, order = CLASSES[c]
        return remote(
            atm.at[part, pl.ds(start, size)], gathered[c].at[offset - 1, part],
            ag_s.at[c, i], ag_r.at[c, i], peer(order[0], offset),
        )

    def forward(c, i, origin, part):
        return remote(
            gathered[c].at[origin - 1, part], gathered[c].at[1, part],
            ag_s.at[c, i], ag_r.at[c, i], peer(CLASSES[c][2][0], origin),
        )

    rings = [[direct(c, 0, 1, low), direct(c, 1, 3, high)] for c in range(3)]
    owns = []
    for c, (start, size, _) in enumerate(CLASSES):
        own = pltpu.make_async_copy(atm.at[:, pl.ds(start, size)], kept[c], own_sem.at[c])
        own.start()
        owns.append(own)

    def edges(side, slot, target, src, dst):
        return (
            copier(src, dst, edge_s.at[0, side], edge_r.at[0, slot], target),
            copier(mask, masks.at[slot], edge_s.at[1, side], edge_r.at[1, slot], target),
        )

    last = state.shape[0] - 1
    wide = state.shape[1]
    to_before = edges(0, 1, before, state.at[:, pl.ds(0, 8)], east)
    to_after = edges(1, 0, after, state.at[:, pl.ds(wide - 8, 8)], west)
    to_below = edges(2, 3, below, state.at[0], north)
    to_fold = edges(3, 3, above, state.at[last], north)
    to_above = edges(3, 2, above, state.at[last], south)
    for copy in to_before + to_after:
        copy.start()
    for case, group in ((has_below, to_below), (is_top, to_fold), (jnp.logical_not(is_top), to_above)):

        @pl.when(case)
        def _():
            for copy in group:
                copy.start()

    asks, mids, p3s = [], [], []
    for c, (_, _, order) in enumerate(CLASSES):
        local = pltpu.make_async_copy(ask, first[c].at[0], ask_sem.at[c])
        local.start()
        asks.append([local])
        for lane in range(1, RING * CORES):
            o3, flip = lane // CORES, lane % CORES
            asks[c].append(
                remote(ask, first[c].at[lane], ask_s.at[c, lane], ask_r.at[c, lane], peer(order[2], -o3, flip))
            )
    for c in range(3):
        rings[c] += [direct(c, 2, 1, high), direct(c, 3, 3, low)]
    for c, (_, _, order) in enumerate(CLASSES):
        for copy in asks[c]:
            copy.wait()
        mids.append(
            [remote(first[c], second[c].at[o], mid_s.at[c, o], mid_r.at[c, o], peer(order[1], -o)) for o in FAR]
        )
        keep = pltpu.make_async_copy(first[c], table.at[c, 0], smem_sem.at[c, 0])
        keep.start()
        mids[c].append(keep)
    for c in range(3):
        for copy in rings[c][:2]:
            copy.wait()
        rings[c] = rings[c][2:] + [forward(c, 4, 1, low), forward(c, 5, 3, high)]
    keeps = []
    for c in range(3):
        for copy in mids[c]:
            copy.wait()
        for o in FAR:
            keep = pltpu.make_async_copy(second[c].at[o], table.at[c, o], smem_sem.at[c, o])
            keep.start()
            keeps.append(keep)
    for keep in keeps:
        keep.wait()

    def pack(c, o2, origins):
        order = CLASSES[c][2]

        def body(lane, carry):
            o3, flip = lane // CORES, lane % CORES
            for o1 in origins:
                for rank in range(2):
                    at = relative({order[0]: o1, order[1]: o2, order[2]: o3}, flip)
                    which = table[c, o2, lane, rank, at]
                    sent[c][o2, o1, lane, rank] = kept[c][which] if o1 == 0 else gathered[c][o1 - 1, which]
            return carry

        lax.fori_loop(0, RING * CORES, body, 0)

    def send2(c, o2, origins):
        order = CLASSES[c][2]
        part = pl.ds(origins[0], len(origins))
        i = 0 if origins[0] == 0 else 1
        return remote(
            sent[c].at[o2, part], relayed[c].at[o2, part], p2_s.at[c, o2, i], p2_r.at[c, o2, i],
            peer(order[1], o2),
        )

    def send3(c, o2):
        start, size, order = CLASSES[c]
        source = sent[c] if o2 == 0 else relayed[c]
        for lane in range(RING * CORES):
            o3, flip = lane // CORES, lane % CORES
            at = {order[0]: slice(None), order[1]: o2, order[2]: o3}
            dst = final.at[at["x"], flip, at["z"], at["y"], :, pl.ds(start, size)]
            src = source.at[o2, :, lane]
            if lane == 0:
                copy = pltpu.make_async_copy(src, dst, p3_s.at[c, o2, 0])
                copy.start()
                p3s.append(copy)
            else:
                p3s.append(
                    remote(src, dst, p3_s.at[c, o2, lane], p3_r.at[c, o2, lane], peer(order[2], o3, flip))
                )

    pending = {(c, o2): [] for c in range(3) for o2 in FAR}
    near, rest = (0,), (1, 2, 3)
    for owner in owns:
        owner.wait()
    last_step = None
    for origins in (near, rest):
        if origins is rest:
            for c in range(3):
                for copy in rings[c]:
                    copy.wait()
        for o2 in FAR:
            for c in range(3):
                pack(c, o2, origins)
                if last_step is not None:
                    pending[last_step[:2]].append(send2(*last_step))
                last_step = (c, o2, origins)
    for c in range(3):
        pack(c, 0, near + rest)
        if c == 0:
            pending[last_step[:2]].append(send2(*last_step))
        else:
            send3(c - 1, 0)
    for o2 in FAR:
        for c in range(3):
            for copy in pending[c, o2]:
                copy.wait()
            send3(c, o2)
            if (c, o2) == (0, 1):
                send3(2, 0)
    for copy in p3s:
        copy.wait()
    for copy in edges(0, 0, before, state.at[:, pl.ds(0, 8)], west) + edges(1, 1, after, state.at[:, pl.ds(0, 8)], east):
        copy.wait()
    for copy in edges(3, 3, above, state.at[last], north):
        copy.wait()

    @pl.when(has_below)
    def _():
        for copy in edges(2, 2, below, state.at[0], south):
            copy.wait()


def exchange(positions, sources, atm, state, mask):
    dma = pltpu.SemaphoreType.DMA
    tables = RING * CORES
    scratch = [pltpu.VMEM((BLOCKS, size, CHANNELS), jnp.bfloat16) for _, size, _ in CLASSES]
    scratch += [pltpu.VMEM((RING - 1, BLOCKS, size, CHANNELS), jnp.bfloat16) for _, size, _ in CLASSES]
    for _ in range(2):
        scratch += [
            pltpu.VMEM((RING, RING, tables, 2, size, CHANNELS), jnp.bfloat16) for _, size, _ in CLASSES
        ]
    scratch += [pltpu.VMEM((tables, 2, 128), jnp.int32) for _ in CLASSES]
    scratch += [pltpu.VMEM((RING, tables, 2, 128), jnp.int32) for _ in CLASSES]
    scratch += [
        pltpu.VMEM((2, 128), jnp.int32),
        pltpu.SMEM((3, RING, tables, 2, 128), jnp.int32),
        dma((3,)),
        dma((3, tables)),
        dma((3, tables)),
        dma((3, RING)),
        dma((3, RING)),
        dma((3, RING)),
        dma((3,)),
        dma((3, 6)),
        dma((3, 6)),
        dma((3, RING, 2)),
        dma((3, RING, 2)),
        dma((3, RING, tables)),
        dma((3, RING, tables)),
        dma((2, 4)),
        dma((2, 4)),
    ]
    lat, lon = mask.shape
    smem = pl.BlockSpec(memory_space=pltpu.SMEM)
    vmem = pl.BlockSpec(memory_space=pltpu.VMEM)
    free = pl.BlockSpec(memory_space=pl.ANY)
    side = jax.ShapeDtypeStruct((lat, 8, CHANNELS), jnp.bfloat16)
    row = jax.ShapeDtypeStruct((lon, CHANNELS), jnp.bfloat16)
    return pl.pallas_call(
        exchange_kernel,
        out_shape=(
            jax.ShapeDtypeStruct((RING, CORES, RING, RING, 2, ROWS, CHANNELS), jnp.bfloat16),
            side,
            side,
            row,
            row,
            jax.ShapeDtypeStruct((4, lat, lon), jnp.int32),
            jax.ShapeDtypeStruct((1, 128), jnp.int32),
        ),
        in_specs=[smem, smem, free, vmem, vmem],
        out_specs=(free, vmem, vmem, vmem, vmem, vmem, vmem),
        scratch_shapes=scratch,
        compiler_params=pltpu.CompilerParams(
            collective_id=0, has_side_effects=True, vmem_limit_bytes=EXCHANGE_VMEM
        ),
        name="exchange",
    )(positions, sources, atm, state, mask)


def remap_kernel(
    count, positions, sources, firsts, targets, weight, blocks, state, mask, mixing,
    west, east, south, north, masks, out, w_buf, x_buf, total, base, wet, w_sem, x_sem,
):
    live = count[0]
    steps = (live + GROUP - 1) // GROUP

    def slot_of(tile):
        lane, _ = where_from(positions[sources[tile]])
        return lane * 2 + jnp.where(firsts[0, lane] == tile, 0, 1)

    def copies(step, at, started=False):
        first = step * GROUP
        yield pltpu.make_async_copy(weight.at[pl.ds(first, GROUP)], w_buf.at[at], w_sem.at[at])
        for i in range(GROUP):
            slot = slot_of(first + i) if started else 0
            yield pltpu.make_async_copy(blocks.at[slot], x_buf.at[at, i], x_sem.at[at, i])

    def fetch(step):
        @pl.when(step < steps)
        def _():
            for copy in copies(step, lax.rem(step, DEPTH), True):
                copy.start()

    for step in range(DEPTH - 1):
        fetch(step)
    total[...] = jnp.zeros_like(total)
    stencil(state, mask, mixing, west, east, south, north, masks, base, wet)

    def body(step, carry):
        at = lax.rem(step, DEPTH)
        fetch(step + DEPTH - 1)
        for copy in copies(step, at):
            copy.wait()
        zero = jnp.zeros((ROWS, CHANNELS), jnp.bfloat16)
        right = []
        for i in range(GROUP):
            tile = step * GROUP + i
            target = jnp.where(tile < live, targets[tile], 2)
            x = x_buf[at, i]
            right.append(
                jnp.concatenate([jnp.where(target == b, x, zero) for b in range(2)], axis=1)
            )
        left = jnp.concatenate([w_buf[at, i] for i in range(GROUP)], axis=1)
        total[...] += jnp.dot(
            left, jnp.concatenate(right, axis=0), preferred_element_type=jnp.float32
        )
        return carry

    lax.fori_loop(0, steps, body, 0)
    lats, lons, _ = state.shape
    for i in range(lats):
        row = i * lons % ROWS
        b = i * lons // ROWS
        forcing = total[row : row + lons, b * CHANNELS : (b + 1) * CHANNELS]
        out[i] = (base[i] + wet[i] * forcing).astype(out.dtype)


def stencil(state, mask, mixing, west, east, south, north, masks, base, wet):
    gy, n_gy = lax.axis_index("gy"), lax.axis_size("gy")
    lats, lons, channels = state.shape
    shape = (lons, channels)

    def columns(part):
        turned = jnp.transpose(part.astype(jnp.float32))
        return [jnp.broadcast_to(turned[:, i : i + 1], shape) for i in range(part.shape[0])]

    lon = lax.broadcasted_iota(jnp.int32, shape, 0)
    reverse = jnp.where(
        lax.broadcasted_iota(jnp.int32, (lons, lons), 0) + lax.broadcasted_iota(jnp.int32, (lons, lons), 1)
        == lons - 1,
        1.0,
        0.0,
    )

    def flip(part):
        return jnp.dot(
            reverse, part, preferred_element_type=jnp.float32, precision=lax.Precision.HIGHEST
        )

    is_top = gy == n_gy - 1
    wets = columns(mask[...])
    west_wets, east_wets = columns(masks[0]), columns(masks[1])
    south_wet = jnp.where(gy == 0, 0.0, columns(masks[2])[lats - 1])
    from_north = columns(masks[3])
    north_wet = jnp.where(is_top, flip(from_north[lats - 1]), from_north[0])
    south_state = jnp.where(gy == 0, 0.0, south[...].astype(jnp.float32))
    north_plain = north[...].astype(jnp.float32)
    north_state = jnp.where(is_top, flip(north_plain), north_plain)
    states = [state[i].astype(jnp.float32) for i in range(lats)]
    scale = mixing[...]
    for i in range(lats):
        center = states[i]
        from_west = jnp.broadcast_to(west[i].astype(jnp.float32)[-1:], shape)
        from_east = jnp.broadcast_to(east[i].astype(jnp.float32)[:1], shape)
        sides = (
            (
                jnp.where(lon == 0, from_west, pltpu.roll(center, 1, 0)),
                jnp.where(lon == 0, pltpu.roll(west_wets[i], 1, 0), pltpu.roll(wets[i], 1, 0)),
            ),
            (
                jnp.where(lon == lons - 1, from_east, pltpu.roll(center, lons - 1, 0)),
                jnp.where(
                    lon == lons - 1, pltpu.roll(east_wets[i], lons - 1, 0), pltpu.roll(wets[i], lons - 1, 0)
                ),
            ),
            (south_state, south_wet) if i == 0 else (states[i - 1], wets[i - 1]),
            (north_state, north_wet) if i == lats - 1 else (states[i + 1], wets[i + 1]),
        )
        diffusion = jnp.zeros_like(center)
        for side_state, side_wet in sides:
            diffusion = diffusion + side_wet * (side_state - center)
        wet[i] = wets[i]
        base[i] = wets[i] * (center + scale * diffusion)


def remap(count, positions, sources, firsts, targets, weight, blocks, state, mask, mixing, halo):
    smem = pl.BlockSpec(memory_space=pltpu.SMEM)
    vmem = pl.BlockSpec(memory_space=pltpu.VMEM)
    hbm = pl.BlockSpec(memory_space=pl.ANY)
    dma = pltpu.SemaphoreType.DMA
    return pl.pallas_call(
        remap_kernel,
        out_shape=jax.ShapeDtypeStruct(state.shape, state.dtype),
        in_specs=[smem, smem, smem, smem, smem, hbm, hbm] + [vmem] * 8,
        out_specs=vmem,
        scratch_shapes=[
            pltpu.VMEM((DEPTH, GROUP, ROWS, ROWS), jnp.bfloat16),
            pltpu.VMEM((DEPTH, GROUP, ROWS, CHANNELS), jnp.bfloat16),
            pltpu.VMEM((ROWS, 2 * CHANNELS), jnp.float32),
            pltpu.VMEM(state.shape, jnp.float32),
            pltpu.VMEM(state.shape, jnp.float32),
            dma((DEPTH,)),
            dma((DEPTH, GROUP)),
        ],
        compiler_params=pltpu.CompilerParams(vmem_limit_bytes=56 * 2**20),
        name="remap",
    )(count, positions, sources, firsts, targets, weight, blocks, state, mask, mixing, *halo)


def local(atm_fields, atm_pos, tile_src, tile_tgt, tile_count, tile_weight, ocean_state, land_mask, mixing):
    blocks, west, east, south, north, masks, firsts = exchange(
        atm_pos, tile_src, atm_fields.reshape(BLOCKS, ROWS, CHANNELS), ocean_state, land_mask
    )
    return remap(
        tile_count,
        atm_pos,
        tile_src,
        firsts,
        tile_tgt,
        tile_weight,
        blocks.reshape(256, ROWS, CHANNELS),
        ocean_state,
        land_mask,
        mixing.reshape(1, CHANNELS),
        (west, east, south, north, masks),
    )


def solution(mesh):
    both = ("gx", "gy")
    in_specs = (
        P(both, None),
        P(),
        P(both),
        P(both),
        P(both),
        P(both, None, None),
        P("gy", "gx", None),
        P("gy", "gx"),
        P(),
    )
    return jax.shard_map(
        local, mesh=mesh, in_specs=in_specs, out_specs=P("gy", "gx", None), check_vma=False
    )
```

time: 238 us -> 172 us (0.72)
  Pallas kernels: 209 us -> 170 us
  local copies, waits for them, and re-layouts: 12.1 us -> 0 us
  starting transfers between devices: 9.65 us -> 0 us
  other arithmetic: 3.71 us -> 0 us
    pallas_call x2, Pallas kernels: 209 us -> 170 us  [the longest x1 157 us: exchange(): pl.pallas_call(exchange_kernel, out_shape=(jax.ShapeDtypeStruct((RING, CO...]
    ppermute x5 -> x0, starting transfers between devices: 9.65 us -> none  [the longest x1 3.98 us: local(): south = lax.ppermute(top, 'gy', line_up)]
    unnamed x12 -> x0, local copies, waits for them, and re-layouts: 5.78 us -> none
    slice x6 -> x0, local copies, waits for them, and re-layouts: 3.07 us -> none  [the longest x2 1.09 us: around(): values[:, 1:]]
  transfers between devices with their start and end apart: 5 -> 0, of which waited for: 0 -> 0; matrix products, arithmetic and copies ran while one was open for 3% -> 0% of each run, Pallas kernels for 89% -> 0%
where the time goes in v2:
time: 172 us; the launch traced here: 171 us
  Pallas kernels  170 us (99%)
    pallas_call x1, Pallas kernels, exchange(): pl.pallas_call(exchange_kernel, out_shape=(jax.ShapeDtypeStruct((RING, CO...  157 us
    pallas_call x1, Pallas kernels, remap(): pl.pallas_call(remap_kernel, out_shape=jax.ShapeDtypeStruct(state.shape,...  13.5 us

profile of v2, /device:TPU:1, one launch (start us, length us, event | category | flops | bytes accessed | tf_op | source)
XLA Modules:
  0.0 170.9 jit_solution(14511944119345316631)
XLA Ops:
  0.7 156.7 %exchange.1 = (bf16[4,2,4,4,2,256,128]{6,5,4,3,2,1,0:T(8,128)(2,1)}, bf16[16,8,128]{2,1,0:T(8,128)(2,1)}, bf16[16,8,128]{2,1,0:T(8,128)(2,1)}, bf16[32,128]{1,0:...) custom-call(s32[3072]{0:T(1024)} %positions.3, s32[160]{0:T(256)} %sources.3, ...), custom_call_target="tpu_custom_call" | custom-call | tf_op jit(solution)/shard_map/exchange/pallas_call | solution.py:306
  157.4 13.5 %remap.1 = bf16[16,32,128]{2,1,0:T(8,128)(2,1)} custom-call(s32[1]{0:T(128)S(6)} %copy.10.count, s32[3072]{0:T(1024)} %positions.3, s32[160]{0:T(256)} %sources.3, s32[1,128]{1,0:T(1,128)} %get-tuple-element.12.firsts, s32[160]{0:T(256)} %targets.1, bf16[160,256,256]{2,1,0:T(8,128)(2,1)} %weight.1, bf16[256,256,128]{2,1,0:T(8,128)(2,1)} %bitcast.3, ...), custom_call_target="tpu_custom_call" | custom-call | tf_op jit(solution)/shard_map/remap/pallas_call | solution.py:448

commit v3 on v2

--- a/solution.py
+++ b/solution.py
@@ -16,6 +16,8 @@
 CLASSES = ((0, 96, "xyz"), (96, 80, "yzx"), (176, 80, "zxy"))
 FAR = (1, 3, 2)
 GROUP = 8
+LIST = 48
+NOBODY = 31
 DEPTH = 4
 EXCHANGE_VMEM = 56 * 2**20
 
@@ -324,6 +326,387 @@
     )(positions, sources, atm, state, mask)
 
 
+def lean_kernel(
+    count, positions, sources, atm, state, mask,
+    final, west, east, south, north, masks, firsts, flag, *scratch
+):
+    kept, gathered, sent, out3, first = (scratch[3 * i : 3 * i + 3] for i in range(5))
+    relayed = [scratch[15 + 3 * c : 18 + 3 * c] for c in range(3)]
+    (ask, needs, spots, lists, heard, over1, over2, over3, over1_in, over2_in, over3_in,
+     table, spot_table, list_table, ask_sem, ask_s, ask_r, list_s, list_r, smem_sem, own_sem,
+     ag_s, ag_r, p2_s, p2_r, p3_s, p3_r, edge_s, edge_r, over_s, over_r) = scratch[24:]
+
+    barrier = pltpu.get_barrier_semaphore()
+    neighbours = [(a, o, f) for a in "xyz" for o in (1, 2, 3) for f in (0, 1)] + [("x", 0, 1)]
+    for axis, offset, flip in neighbours:
+        pl.semaphore_signal(barrier, 1, device_id=peer(axis, offset, flip), device_id_type=MESH)
+    gx, gy = lax.axis_index("gx"), lax.axis_index("gy")
+    n_gx, n_gy = lax.axis_size("gx"), lax.axis_size("gy")
+    is_top = gy == n_gy - 1
+    before, after = ((gx + n_gx - 1) % n_gx, gy), ((gx + 1) % n_gx, gy)
+    above = (jnp.where(is_top, n_gx - 1 - gx, gx), jnp.where(is_top, gy, gy + 1))
+    below = (gx, gy - 1)
+    has_below = gy > 0
+    for target in (before, after, above):
+        pl.semaphore_signal(barrier, 1, device_id=target, device_id_type=MESH)
+
+    @pl.when(has_below)
+    def _():
+        pl.semaphore_signal(barrier, 1, device_id=below, device_id_type=MESH)
+
+    lane_of = lax.broadcasted_iota(jnp.int32, (1, 128), 1)
+    zero = jnp.zeros((1, 128), jnp.int32)
+    live = count[0]
+
+    def claim(step, carry):
+        taken, ask0, ask1, leader = carry
+        for i in range(8):
+            tile = step * 8 + i
+            lane, block = where_from(positions[sources[tile]])
+            mine = lane_of == jnp.where(tile < live, lane, 128)
+            free = mine & (taken == 0)
+            ask0 = jnp.where(free, block, ask0)
+            leader = jnp.where(free, tile, leader)
+            ask1 = jnp.where(mine, jnp.where(free, ask1, block), ask1)
+            taken = jnp.where(mine, 1, taken)
+        return taken, ask0, ask1, leader
+
+    _, ask0, ask1, leader = lax.fori_loop(
+        0, sources.shape[0] // 8, claim, (zero, zero + NOBODY, zero + NOBODY, zero)
+    )
+    ask[0:1] = ask0
+    ask[1:2] = ask1
+    firsts[...] = leader
+    pl.semaphore_wait(barrier, len(neighbours) + 3 + jnp.where(has_below, 1, 0))
+
+    def copier(src, dst, send, recv, target):
+        return pltpu.make_async_remote_copy(
+            src_ref=src, dst_ref=dst, send_sem=send, recv_sem=recv, device_id=target, device_id_type=MESH
+        )
+
+    def remote(*parts):
+        copy = copier(*parts)
+        copy.start()
+        return copy
+
+    def keep(src, dst, sem):
+        copy = pltpu.make_async_copy(src, dst, sem)
+        copy.start()
+        return copy
+
+    half = BLOCKS // 2
+    low, high = pl.ds(0, half), pl.ds(half, half)
+
+    def direct(c, i, offset, part):
+        start, size, order = CLASSES[c]
+        return remote(
+            atm.at[part, pl.ds(start, size)], gathered[c].at[offset, part],
+            ag_s.at[c, i], ag_r.at[c, i], peer(order[0], offset),
+        )
+
+    def forward(c, i, origin, part):
+        return remote(
+            gathered[c].at[origin, part], gathered[c].at[2, part],
+            ag_s.at[c, i], ag_r.at[c, i], peer(CLASSES[c][2][0], origin),
+        )
+
+    rings = [[direct(c, 0, 1, low), direct(c, 1, 3, high)] for c in range(3)]
+    owns = []
+    for c, (start, size, _) in enumerate(CLASSES):
+        owns.append(keep(atm.at[:, pl.ds(start, size)], kept[c], own_sem.at[c, 0]))
+        rings[c].append(keep(atm.at[:, pl.ds(start, size)], gathered[c].at[0], own_sem.at[c, 1]))
+
+    def edges(side, slot, target, src, dst):
+        return (
+            copier(src, dst, edge_s.at[0, side], edge_r.at[0, slot], target),
+            copier(mask, masks.at[slot], edge_s.at[1, side], edge_r.at[1, slot], target),
+        )
+
+    last = state.shape[0] - 1
+    wide = state.shape[1]
+    to_before = edges(0, 1, before, state.at[:, pl.ds(0, 8)], east)
+    to_after = edges(1, 0, after, state.at[:, pl.ds(wide - 8, 8)], west)
+    to_below = edges(2, 3, below, state.at[0], north)
+    to_fold = edges(3, 3, above, state.at[last], north)
+    to_above = edges(3, 2, above, state.at[last], south)
+    for copy in to_before + to_after:
+        copy.start()
+    for case, group in ((has_below, to_below), (is_top, to_fold), (jnp.logical_not(is_top), to_above)):
+
+        @pl.when(case)
+        def _():
+            for copy in group:
+                copy.start()
+
+    asks = []
+    for c, (_, _, order) in enumerate(CLASSES):
+        asks.append([keep(ask, first[c].at[0], ask_sem.at[c])])
+        for lane in range(1, RING * CORES):
+            o3, flip = lane // CORES, lane % CORES
+            asks[c].append(
+                remote(ask, first[c].at[lane], ask_s.at[c, lane], ask_r.at[c, lane], peer(order[2], -o3, flip))
+            )
+    for c in range(3):
+        rings[c] += [direct(c, 2, 1, high), direct(c, 3, 3, low)]
+
+    def wanted(c, o1, o2, lane, rank):
+        order = CLASSES[c][2]
+        o3, flip = lane // CORES, lane % CORES
+        return table[c, lane, rank, relative({order[0]: o1, order[1]: o2, order[2]: o3}, flip)]
+
+    keeps = []
+    for c in range(3):
+        for copy in asks[c]:
+            copy.wait()
+        keeps.append(keep(first[c], table.at[c], smem_sem.at[0, c]))
+    needs[...] = jnp.zeros_like(needs)
+    for c in range(3):
+        keeps[c].wait()
+
+        def mark(lane, seen):
+            seen = list(seen)
+            for o2 in FAR:
+                for o1 in range(RING):
+                    for rank in range(2):
+                        key = o1 * 32 + wanted(c, o1, o2, lane, rank)
+                        seen[o2 - 1] = jnp.where(lane_of == key, 1, seen[o2 - 1])
+            return tuple(seen)
+
+        seen = lax.fori_loop(0, RING * CORES, mark, (zero, zero, zero))
+        for o2 in FAR:
+            row = c * 3 + o2 - 1
+            needs[row : row + 1] = jnp.where((lane_of & 31) < BLOCKS, seen[o2 - 1], 0)
+
+    need = needs[...]
+    upper = lax.broadcasted_iota(jnp.int32, (128, 128), 0) < lax.broadcasted_iota(jnp.int32, (128, 128), 1)
+    spot = jnp.dot(
+        need.astype(jnp.float32).astype(jnp.bfloat16),
+        jnp.where(upper, 1.0, 0.0).astype(jnp.bfloat16),
+        preferred_element_type=jnp.float32,
+    ).astype(jnp.int32)
+    over1[...] = jnp.where((need > 0) & (spot >= LIST), 1, 0)
+    spots[...] = jnp.clip(spot, 0, LIST - 1)
+    keys = lax.broadcasted_iota(jnp.int32, (8, 128), 1).astype(jnp.float32).astype(jnp.bfloat16)
+    place = lax.broadcasted_iota(jnp.int32, (128, 128), 0)
+    for row in range(9):
+        mine = (spot[row : row + 1] == place) & (need[row : row + 1] > 0)
+        lists[row] = lax.dot_general(
+            keys,
+            jnp.where(mine, 1.0, 0.0).astype(jnp.bfloat16),
+            (((1,), (1,)), ((), ())),
+            preferred_element_type=jnp.float32,
+        ).astype(jnp.int32)
+
+    def pack3(c, o2, origins):
+        def body(lane, carry):
+            for o1 in origins:
+                for rank in range(2):
+                    which = wanted(c, o1, o2, lane, rank) & 31
+                    if o2:
+                        at = jnp.clip(spot_table[c * 3 + o2 - 1, o1 * 32 + which], 0, LIST - 1)
+                        block = relayed[c][o2 - 1][at]
+                    elif o1 == 0:
+                        block = kept[c][jnp.minimum(which, BLOCKS - 1)]
+                    else:
+                        block = gathered[c][o1, jnp.minimum(which, BLOCKS - 1)]
+                    out3[c][o2, lane, o1, rank] = block
+            return carry
+
+        lax.fori_loop(0, RING * CORES, body, 0)
+
+    p3s = []
+
+    def send3(c, o2, origins, part):
+        start, size, order = CLASSES[c]
+        span = pl.ds(origins[0], len(origins))
+        for lane in range(RING * CORES):
+            o3, flip = lane // CORES, lane % CORES
+            at = {order[0]: span, order[1]: o2, order[2]: o3}
+            dst = final.at[at["x"], flip, at["z"], at["y"], :, pl.ds(start, size)]
+            src = out3[c].at[o2, lane, span]
+            if lane == 0:
+                p3s.append(keep(src, dst, p3_s.at[c, part, 0]))
+            else:
+                p3s.append(
+                    remote(src, dst, p3_s.at[c, part, lane], p3_r.at[c, part, lane], peer(order[2], o3, flip))
+                )
+
+    near, rest, every = (0,), (1, 2, 3), (0, 1, 2, 3)
+    spot_keep = keep(spots, spot_table, smem_sem.at[1, 0])
+    for owner in owns:
+        owner.wait()
+    pack3(0, 0, near)
+    tells = []
+    for c, (_, _, order) in enumerate(CLASSES):
+        for o2 in FAR:
+            row = c * 3 + o2 - 1
+            tells.append(
+                remote(lists.at[row], heard.at[row], list_s.at[row], list_r.at[row], peer(order[1], -o2))
+            )
+    circle = [(o, f) for o in range(RING) for f in range(CORES) if o or f]
+    votes = [
+        remote(over1, over1_in.at[i], over_s.at[i], over_r.at[i], peer("x", o, f))
+        for i, (o, f) in enumerate(circle)
+    ]
+    for c in range(3):
+        for copy in rings[c][:3]:
+            copy.wait()
+        rings[c] = rings[c][3:] + [forward(c, 4, 1, low), forward(c, 5, 3, high)]
+    pack3(1, 0, near)
+    send3(0, 0, near, 4)
+    pack3(2, 0, near)
+    send3(1, 0, near, 4)
+    for row, copy in enumerate(tells):
+        copy.wait()
+    list_keep = keep(heard, list_table, smem_sem.at[1, 1])
+    send3(2, 0, near, 4)
+    list_keep.wait()
+    spot_keep.wait()
+    for c in range(3):
+        for copy in rings[c]:
+            copy.wait()
+
+    def pack2(c, o2):
+        row = c * 3 + o2 - 1
+
+        def body(step, carry):
+            for i in range(8):
+                slot = step * 8 + i
+                key = list_table[row, 0, slot]
+                origin = lax.shift_right_logical(key, 5)
+                sent[c][o2 - 1, slot] = gathered[c][origin & 3, jnp.minimum(key & 31, BLOCKS - 1)]
+            return carry
+
+        lax.fori_loop(0, LIST // 8, body, 0)
+
+    def send2(c, o2):
+        return remote(
+            sent[c].at[o2 - 1], relayed[c][o2 - 1], p2_s.at[c, o2 - 1], p2_r.at[c, o2 - 1],
+            peer(CLASSES[c][2][1], o2),
+        )
+
+    steps = [(c, o2) for o2 in FAR for c in range(3)]
+    pending = {}
+    for i, step in enumerate(steps):
+        pack2(*step)
+        if i:
+            pending[steps[i - 1]] = send2(*steps[i - 1])
+    pack3(0, 0, rest)
+    pending[steps[-1]] = send2(*steps[-1])
+    for copy in votes:
+        copy.wait()
+    over2[...] = functools.reduce(jnp.maximum, [over1_in[i] for i in range(len(circle))], over1[...])
+    pack3(1, 0, rest)
+    send3(0, 0, rest, 0)
+    pack3(2, 0, rest)
+    send3(1, 0, rest, 0)
+    votes = [
+        remote(over2, over2_in.at[o - 1], over_s.at[7 + o - 1], over_r.at[7 + o - 1], peer("y", o)) for o in FAR
+    ]
+    send3(2, 0, rest, 0)
+    for i, (c, o2) in enumerate(steps):
+        pending[c, o2].wait()
+        pack3(c, o2, every)
+        send3(c, o2, every, o2)
+        if i == 2:
+            for copy in votes:
+                copy.wait()
+            over3[...] = functools.reduce(jnp.maximum, [over2_in[k] for k in range(3)], over2[...])
+        if i == 3:
+            votes = [
+                remote(over3, over3_in.at[o - 1], over_s.at[10 + o - 1], over_r.at[10 + o - 1], peer("z", o))
+                for o in FAR
+            ]
+    for copy in votes:
+        copy.wait()
+    verdict = functools.reduce(jnp.maximum, [over3_in[k] for k in range(3)], over3[...])
+    flag[0] = jnp.max(verdict)
+    for copy in p3s:
+        copy.wait()
+    for copy in edges(0, 0, before, state.at[:, pl.ds(0, 8)], west) + edges(1, 1, after, state.at[:, pl.ds(0, 8)], east):
+        copy.wait()
+    for copy in edges(3, 3, above, state.at[last], north):
+        copy.wait()
+
+    @pl.when(has_below)
+    def _():
+        for copy in edges(2, 2, below, state.at[0], south):
+            copy.wait()
+
+
+def lean_exchange(count, positions, sources, atm, state, mask):
+    dma = pltpu.SemaphoreType.DMA
+    tables = RING * CORES
+    sizes = [size for _, size, _ in CLASSES]
+    scratch = [pltpu.VMEM((BLOCKS, size, CHANNELS), jnp.bfloat16) for size in sizes]
+    scratch += [pltpu.VMEM((RING, BLOCKS, size, CHANNELS), jnp.bfloat16) for size in sizes]
+    scratch += [pltpu.VMEM((3, LIST, size, CHANNELS), jnp.bfloat16) for size in sizes]
+    scratch += [pltpu.VMEM((RING, tables, RING, 2, size, CHANNELS), jnp.bfloat16) for size in sizes]
+    scratch += [pltpu.VMEM((tables, 2, 128), jnp.int32) for _ in sizes]
+    for size in sizes:
+        scratch += [pltpu.VMEM((LIST, size, CHANNELS), jnp.bfloat16) for _ in range(3)]
+    votes = pltpu.VMEM((16, 128), jnp.int32)
+    scratch += [
+        pltpu.VMEM((2, 128), jnp.int32),
+        votes,
+        votes,
+        pltpu.VMEM((9, 8, 128), jnp.int32),
+        pltpu.VMEM((9, 8, 128), jnp.int32),
+        votes,
+        votes,
+        votes,
+        pltpu.VMEM((7, 16, 128), jnp.int32),
+        pltpu.VMEM((3, 16, 128), jnp.int32),
+        pltpu.VMEM((3, 16, 128), jnp.int32),
+        pltpu.SMEM((3, tables, 2, 128), jnp.int32),
+        pltpu.SMEM((16, 128), jnp.int32),
+        pltpu.SMEM((9, 8, 128), jnp.int32),
+        dma((3,)),
+        dma((3, tables)),
+        dma((3, tables)),
+        dma((9,)),
+        dma((9,)),
+        dma((2, 3)),
+        dma((3, 2)),
+        dma((3, 6)),
+        dma((3, 6)),
+        dma((3, 3)),
+        dma((3, 3)),
+        dma((3, RING + 1, tables)),
+        dma((3, RING + 1, tables)),
+        dma((2, 4)),
+        dma((2, 4)),
+        dma((13,)),
+        dma((13,)),
+    ]
+    lat, lon = mask.shape
+    smem = pl.BlockSpec(memory_space=pltpu.SMEM)
+    vmem = pl.BlockSpec(memory_space=pltpu.VMEM)
+    free = pl.BlockSpec(memory_space=pl.ANY)
+    side = jax.ShapeDtypeStruct((lat, 8, CHANNELS), jnp.bfloat16)
+    row = jax.ShapeDtypeStruct((lon, CHANNELS), jnp.bfloat16)
+    return pl.pallas_call(
+        lean_kernel,
+        out_shape=(
+            jax.ShapeDtypeStruct((RING, CORES, RING, RING, 2, ROWS, CHANNELS), jnp.bfloat16),
+            side,
+            side,
+            row,
+            row,
+            jax.ShapeDtypeStruct((4, lat, lon), jnp.int32),
+            jax.ShapeDtypeStruct((1, 128), jnp.int32),
+            jax.ShapeDtypeStruct((1,), jnp.int32),
+        ),
+        in_specs=[smem, smem, smem, free, vmem, vmem],
+        out_specs=(free, vmem, vmem, vmem, vmem, vmem, vmem, smem),
+        scratch_shapes=scratch,
+        compiler_params=pltpu.CompilerParams(
+            collective_id=1, has_side_effects=True, vmem_limit_bytes=EXCHANGE_VMEM
+        ),
+        name="lean_exchange",
+    )(count, positions, sources, atm, state, mask)
+
+
 def remap_kernel(
     count, positions, sources, firsts, targets, weight, blocks, state, mask, mixing,
     west, east, south, north, masks, out, w_buf, x_buf, total, base, wet, w_sem, x_sem,
@@ -465,21 +848,20 @@
 
 
 def local(atm_fields, atm_pos, tile_src, tile_tgt, tile_count, tile_weight, ocean_state, land_mask, mixing):
-    blocks, west, east, south, north, masks, firsts = exchange(
-        atm_pos, tile_src, atm_fields.reshape(BLOCKS, ROWS, CHANNELS), ocean_state, land_mask
-    )
-    return remap(
-        tile_count,
-        atm_pos,
-        tile_src,
-        firsts,
-        tile_tgt,
-        tile_weight,
-        blocks.reshape(256, ROWS, CHANNELS),
-        ocean_state,
-        land_mask,
-        mixing.reshape(1, CHANNELS),
-        (west, east, south, north, masks),
+    atm = atm_fields.reshape(BLOCKS, ROWS, CHANNELS)
+
+    def finish(blocks, west, east, south, north, masks, firsts):
+        return remap(
+            tile_count, atm_pos, tile_src, firsts, tile_tgt, tile_weight, blocks.reshape(256, ROWS, CHANNELS),
+            ocean_state, land_mask, mixing.reshape(1, CHANNELS), (west, east, south, north, masks),
+        )
+
+    *parts, over = lean_exchange(tile_count, atm_pos, tile_src, atm, ocean_state, land_mask)
+    return lax.cond(
+        over[0] > 0,
+        lambda parts: finish(*exchange(atm_pos, tile_src, atm, ocean_state, land_mask)),
+        lambda parts: finish(*parts),
+        parts,
     )
 
 

time: 172 us -> 162 us (0.942)
  Pallas kernels: 170 us -> 159 us
    pallas_call x1, Pallas kernels: 157 us -> 145 us  [lean_exchange(): pl.pallas_call(lean_kernel, out_shape=(jax.ShapeDtypeStruct((RING, CORES,...]
where the time goes in v3:
time: 162 us; the launch traced here: 161 us
  Pallas kernels  159 us (98%)
    pallas_call x1, Pallas kernels, lean_exchange(): pl.pallas_call(lean_kernel, out_shape=(jax.ShapeDtypeStruct((RING, CORES,...  145 us
    pallas_call x1, Pallas kernels, remap(): pl.pallas_call(remap_kernel, out_shape=jax.ShapeDtypeStruct(state.shape,...  14.1 us

profile of v3, /device:TPU:1, one launch (start us, length us, event | category | flops | bytes accessed | tf_op | source)
XLA Modules:
  0.0 161.3 jit_solution(7266767371963440384)
XLA Ops:
  0.7 145.2 %lean_exchange.1 = (bf16[4,2,4,4,2,256,128]{6,5,4,3,2,1,0:T(8,128)(2,1)}, bf16[16,8,128]{2,1,0:T(8,128)(2,1)S(1)}, bf16[16,8,128]{2,1,0:T(8,128)(2,1)S(1)}, bf16...) custom-call(s32[1]{0:T(128)S(6)} %copy.14.count, ...), custom_call_target="tpu_custom_call" | custom-call | tf_op jit(solution)/shard_map/lean_exchange/pallas_call | solution.py:688
  146.6 14.1 %conditional.1 = (bf16[16,32,128]{2,1,0:T(8,128)(2,1)S(1)}) conditional(s32[]{:T(128)} %bitcast.5, (bf16[4,2,4,4,2,256,128]{6,5,4,3,2,1,0:T(8,128)(2,1)}, f32[128]{0:T(128)}, s32[1]{0:T(128)}, s32[3072]{0:T(1024)}, s32[160]{0:T(256)}, /*index=5*/s32[1,128]{1,0:T(1,128)S(1)}, s32[160]{0:T(256)}, bf16[160,256,256]{2,1,0:T(8,128)(2,1)}, ...), branch_computations={%region_0.0_spmd, %region_1.0_spmd} | conditional | bytes 8 | solution.py:860
  146.6 14.1 %remap.2 = bf16[16,32,128]{2,1,0:T(8,128)(2,1)S(1)} custom-call(s32[1]{0:T(128)} %get-tuple-element.56.count, s32[3072]{0:T(1024)} %get-tuple-element.57.positions, s32[160]{0:T(256)} %get-tuple-element.58.sources, s32[1,128]{1,0:T(1,128)S(1)} %get-tuple-element.59.firsts, s32[160]{0:T(256)} %get-tuple-element.60.targets, ...), custom_call_target="tpu_custom_call" | custom-call | tf_op jit(solution)/shard_map/cond/branch_0_fun/remap/pallas_call | solution.py:831
  160.7 0.0 copy-start
  160.7 0.6 copy-done
Async XLA Ops:
  160.7 0.7 copy-start

commit v4 on v3

--- a/solution.py
+++ b/solution.py
@@ -13,7 +13,7 @@
 BLOCKS = 24
 RING = 4
 CORES = 2
-CLASSES = ((0, 96, "xyz"), (96, 80, "yzx"), (176, 80, "zxy"))
+CLASSES = ((0, 88, "xyz"), (88, 88, "yzx"), (176, 80, "zxy"))
 FAR = (1, 3, 2)
 GROUP = 8
 LIST = 48
@@ -46,14 +46,23 @@
     return relative({"x": dx, "z": dz, "y": dy}, dk), position - owner * BLOCKS
 
 
+def write_slots(slots, positions, sources, leaders):
+    def body(tile, carry):
+        lane, _ = where_from(positions[sources[tile]])
+        slots[tile] = lane * 2 + jnp.where(leaders[0, lane] == tile, 0, 1)
+        return carry
+
+    lax.fori_loop(0, sources.shape[0], body, 0)
+
+
 def relative(distance, core):
     return ((distance["x"] * CORES + core) * RING + distance["z"]) * RING + distance["y"]
 
 
-def exchange_kernel(positions, sources, atm, state, mask, final, west, east, south, north, masks, firsts, *scratch):
+def exchange_kernel(positions, sources, atm, state, mask, final, west, east, south, north, masks, slots, *scratch):
     kept, gathered, sent, relayed, first, second = (scratch[3 * i : 3 * i + 3] for i in range(6))
     (ask, table, ask_sem, ask_s, ask_r, mid_s, mid_r, smem_sem, own_sem, ag_s, ag_r,
-     p2_s, p2_r, p3_s, p3_r, edge_s, edge_r) = scratch[18:]
+     p2_s, p2_r, p3_s, p3_r, edge_s, edge_r, firsts, leaders, lead_sem) = scratch[18:]
 
     barrier = pltpu.get_barrier_semaphore()
     neighbours = [(a, o, f) for a in "xyz" for o in (1, 2, 3) for f in (0, 1)] + [("x", 0, 1)]
@@ -249,6 +258,10 @@
             pending[last_step[:2]].append(send2(*last_step))
         else:
             send3(c - 1, 0)
+    lead = pltpu.make_async_copy(firsts, leaders, lead_sem)
+    lead.start()
+    lead.wait()
+    write_slots(slots, positions, sources, leaders)
     for o2 in FAR:
         for c in range(3):
             for copy in pending[c, o2]:
@@ -298,6 +311,9 @@
         dma((3, RING, tables)),
         dma((2, 4)),
         dma((2, 4)),
+        pltpu.VMEM((1, 128), jnp.int32),
+        pltpu.SMEM((1, 128), jnp.int32),
+        dma,
     ]
     lat, lon = mask.shape
     smem = pl.BlockSpec(memory_space=pltpu.SMEM)
@@ -314,10 +330,10 @@
             row,
             row,
             jax.ShapeDtypeStruct((4, lat, lon), jnp.int32),
-            jax.ShapeDtypeStruct((1, 128), jnp.int32),
+            jax.ShapeDtypeStruct(sources.shape, jnp.int32),
         ),
         in_specs=[smem, smem, free, vmem, vmem],
-        out_specs=(free, vmem, vmem, vmem, vmem, vmem, vmem),
+        out_specs=(free, vmem, vmem, vmem, vmem, vmem, smem),
         scratch_shapes=scratch,
         compiler_params=pltpu.CompilerParams(
             collective_id=0, has_side_effects=True, vmem_limit_bytes=EXCHANGE_VMEM
@@ -328,13 +344,13 @@
 
 def lean_kernel(
     count, positions, sources, atm, state, mask,
-    final, west, east, south, north, masks, firsts, flag, *scratch
+    final, west, east, south, north, masks, slots, flag, *scratch
 ):
     kept, gathered, sent, out3, first = (scratch[3 * i : 3 * i + 3] for i in range(5))
     relayed = [scratch[15 + 3 * c : 18 + 3 * c] for c in range(3)]
     (ask, needs, spots, lists, heard, over1, over2, over3, over1_in, over2_in, over3_in,
      table, spot_table, list_table, ask_sem, ask_s, ask_r, list_s, list_r, smem_sem, own_sem,
-     ag_s, ag_r, p2_s, p2_r, p3_s, p3_r, edge_s, edge_r, over_s, over_r) = scratch[24:]
+     ag_s, ag_r, p2_s, p2_r, p3_s, p3_r, edge_s, edge_r, over_s, over_r, firsts, leaders, lead_sem) = scratch[24:]
 
     barrier = pltpu.get_barrier_semaphore()
     neighbours = [(a, o, f) for a in "xyz" for o in (1, 2, 3) for f in (0, 1)] + [("x", 0, 1)]
@@ -604,6 +620,8 @@
         remote(over2, over2_in.at[o - 1], over_s.at[7 + o - 1], over_r.at[7 + o - 1], peer("y", o)) for o in FAR
     ]
     send3(2, 0, rest, 0)
+    keep(firsts, leaders, lead_sem).wait()
+    write_slots(slots, positions, sources, leaders)
     for i, (c, o2) in enumerate(steps):
         pending[c, o2].wait()
         pack3(c, o2, every)
@@ -678,11 +696,15 @@
         dma((2, 4)),
         dma((13,)),
         dma((13,)),
+        pltpu.VMEM((1, 128), jnp.int32),
+        pltpu.SMEM((1, 128), jnp.int32),
+        dma,
     ]
     lat, lon = mask.shape
     smem = pl.BlockSpec(memory_space=pltpu.SMEM)
     vmem = pl.BlockSpec(memory_space=pltpu.VMEM)
     free = pl.BlockSpec(memory_space=pl.ANY)
+    hbm = pl.BlockSpec(memory_space=pltpu.HBM)
     side = jax.ShapeDtypeStruct((lat, 8, CHANNELS), jnp.bfloat16)
     row = jax.ShapeDtypeStruct((lon, CHANNELS), jnp.bfloat16)
     return pl.pallas_call(
@@ -694,11 +716,11 @@
             row,
             row,
             jax.ShapeDtypeStruct((4, lat, lon), jnp.int32),
-            jax.ShapeDtypeStruct((1, 128), jnp.int32),
+            jax.ShapeDtypeStruct(sources.shape, jnp.int32),
             jax.ShapeDtypeStruct((1,), jnp.int32),
         ),
-        in_specs=[smem, smem, smem, free, vmem, vmem],
-        out_specs=(free, vmem, vmem, vmem, vmem, vmem, vmem, smem),
+        in_specs=[smem, smem, smem, free, hbm, hbm],
+        out_specs=(free, hbm, hbm, hbm, hbm, hbm, smem, smem),
         scratch_shapes=scratch,
         compiler_params=pltpu.CompilerParams(
             collective_id=1, has_side_effects=True, vmem_limit_bytes=EXCHANGE_VMEM
@@ -708,21 +730,17 @@
 
 
 def remap_kernel(
-    count, positions, sources, firsts, targets, weight, blocks, state, mask, mixing,
+    count, slots, targets, weight, blocks, state, mask, mixing,
     west, east, south, north, masks, out, w_buf, x_buf, total, base, wet, w_sem, x_sem,
 ):
     live = count[0]
     steps = (live + GROUP - 1) // GROUP
 
-    def slot_of(tile):
-        lane, _ = where_from(positions[sources[tile]])
-        return lane * 2 + jnp.where(firsts[0, lane] == tile, 0, 1)
-
     def copies(step, at, started=False):
         first = step * GROUP
         yield pltpu.make_async_copy(weight.at[pl.ds(first, GROUP)], w_buf.at[at], w_sem.at[at])
         for i in range(GROUP):
-            slot = slot_of(first + i) if started else 0
+            slot = slots[first + i] if started else 0
             yield pltpu.make_async_copy(blocks.at[slot], x_buf.at[at, i], x_sem.at[at, i])
 
     def fetch(step):
@@ -823,7 +841,7 @@
         base[i] = wets[i] * (center + scale * diffusion)
 
 
-def remap(count, positions, sources, firsts, targets, weight, blocks, state, mask, mixing, halo):
+def remap(count, slots, targets, weight, blocks, state, mask, mixing, halo):
     smem = pl.BlockSpec(memory_space=pltpu.SMEM)
     vmem = pl.BlockSpec(memory_space=pltpu.VMEM)
     hbm = pl.BlockSpec(memory_space=pl.ANY)
@@ -831,7 +849,7 @@
     return pl.pallas_call(
         remap_kernel,
         out_shape=jax.ShapeDtypeStruct(state.shape, state.dtype),
-        in_specs=[smem, smem, smem, smem, smem, hbm, hbm] + [vmem] * 8,
+        in_specs=[smem, smem, smem, hbm, hbm] + [vmem] * 8,
         out_specs=vmem,
         scratch_shapes=[
             pltpu.VMEM((DEPTH, GROUP, ROWS, ROWS), jnp.bfloat16),
@@ -844,21 +862,21 @@
         ],
         compiler_params=pltpu.CompilerParams(vmem_limit_bytes=56 * 2**20),
         name="remap",
-    )(count, positions, sources, firsts, targets, weight, blocks, state, mask, mixing, *halo)
+    )(count, slots, targets, weight, blocks, state, mask, mixing, *halo)
 
 
 def local(atm_fields, atm_pos, tile_src, tile_tgt, tile_count, tile_weight, ocean_state, land_mask, mixing):
     atm = atm_fields.reshape(BLOCKS, ROWS, CHANNELS)
 
-    def finish(blocks, west, east, south, north, masks, firsts):
+    def finish(blocks, west, east, south, north, masks, slots):
         return remap(
-            tile_count, atm_pos, tile_src, firsts, tile_tgt, tile_weight, blocks.reshape(256, ROWS, CHANNELS),
+            tile_count, slots, tile_tgt, tile_weight, blocks.reshape(256, ROWS, CHANNELS),
             ocean_state, land_mask, mixing.reshape(1, CHANNELS), (west, east, south, north, masks),
         )
 
     *parts, over = lean_exchange(tile_count, atm_pos, tile_src, atm, ocean_state, land_mask)
     return lax.cond(
-        over[0] > 0,
+        over.reshape(()) > 0,
         lambda parts: finish(*exchange(atm_pos, tile_src, atm, ocean_state, land_mask)),
         lambda parts: finish(*parts),
         parts,

time: 162 us -> 158 us (0.975)
  Pallas kernels: 159 us -> 155 us
    pallas_call x1, Pallas kernels: 145 us -> 142 us  [lean_exchange(): pl.pallas_call(lean_kernel, out_shape=(jax.ShapeDtypeStruct((RING, CORES,...]
where the time goes in v4:
time: 158 us; the launch traced here: 157 us
  Pallas kernels  155 us (98%)
    pallas_call x1, Pallas kernels, lean_exchange(): pl.pallas_call(lean_kernel, out_shape=(jax.ShapeDtypeStruct((RING, CORES,...  142 us
    pallas_call x1, Pallas kernels, remap(): pl.pallas_call(remap_kernel, out_shape=jax.ShapeDtypeStruct(state.shape,...  12.7 us

profile of v4, /device:TPU:1, one launch (start us, length us, event | category | flops | bytes accessed | tf_op | source)
XLA Modules:
  0.0 157.1 jit_solution(18398992552502639431)
XLA Ops:
  0.7 142.4 %lean_exchange.1 = (bf16[4,2,4,4,2,256,128]{6,5,4,3,2,1,0:T(8,128)(2,1)}, bf16[16,8,128]{2,1,0:T(8,128)(2,1)S(1)}, bf16[16,8,128]{2,1,0:T(8,128)(2,1)S(1)}, bf16...) custom-call(s32[1]{0:T(128)S(6)} %copy.14.count, ...), custom_call_target="tpu_custom_call" | custom-call | tf_op jit(solution)/shard_map/lean_exchange/pallas_call | solution.py:710
  143.8 12.7 %conditional.1 = (bf16[16,32,128]{2,1,0:T(8,128)(2,1)S(1)}) conditional(s32[]{:T(128)} %bitcast.5, (bf16[4,2,4,4,2,256,128]{6,5,4,3,2,1,0:T(8,128)(2,1)}, f32[128]{0:T(128)}, s32[1]{0:T(128)}, s32[160]{0:T(256)S(1)}, s32[160]{0:T(256)}, /*index=5*/bf16[160,256,256]{2,1,0:T(8,128)(2,1)}, bf16[16,32,128]{2,1,0:T(8,128)(2,1)}, s32[16,32]{1,0:T(8,128)}, ...), branch_computations={%region_0.0_spmd, %region_1.0_spmd} | conditional | bytes 8 | solution.py:878
  143.8 12.7 %remap.2 = bf16[16,32,128]{2,1,0:T(8,128)(2,1)S(1)} custom-call(s32[1]{0:T(128)} %get-tuple-element.52.count, s32[160]{0:T(256)S(1)} %get-tuple-element.53.slots, s32[160]{0:T(256)} %get-tuple-element.54.targets, bf16[160,256,256]{2,1,0:T(8,128)(2,1)} %get-tuple-element.55.weight, bf16[256,256,128]{2,1,0:T(8,128)(2,1)} %bitcast.6, ...), custom_call_target="tpu_custom_call" | custom-call | tf_op jit(solution)/shard_map/cond/branch_0_fun/remap/pallas_call | solution.py:849
  156.5 0.0 copy-start
  156.5 0.6 copy-done
Async XLA Ops:
  156.5 0.7 copy-start

commit v5 on v4

--- a/solution.py
+++ b/solution.py
@@ -14,7 +14,7 @@
 RING = 4
 CORES = 2
 CLASSES = ((0, 88, "xyz"), (88, 88, "yzx"), (176, 80, "zxy"))
-FAR = (1, 3, 2)
+FAR = (2, 1, 3)
 GROUP = 8
 LIST = 48
 NOBODY = 31

time: 158 us -> 158 us (level)
  no operation moved by 1% of the time
where the time goes in v5:
time: 158 us
  Pallas kernels  156 us (99%)
    pallas_call x1, Pallas kernels, lean_exchange(): pl.pallas_call(lean_kernel, out_shape=(jax.ShapeDtypeStruct((RING, CORES,...  142 us
    pallas_call x1, Pallas kernels, remap(): pl.pallas_call(remap_kernel, out_shape=jax.ShapeDtypeStruct(state.shape,...  13.2 us

profile of v5, /device:TPU:1, one launch (start us, length us, event | category | flops | bytes accessed | tf_op | source)
XLA Modules:
  0.0 157.6 jit_solution(14094191768601390493)
XLA Ops:
  0.7 142.4 %lean_exchange.1 = (bf16[4,2,4,4,2,256,128]{6,5,4,3,2,1,0:T(8,128)(2,1)}, bf16[16,8,128]{2,1,0:T(8,128)(2,1)S(1)}, bf16[16,8,128]{2,1,0:T(8,128)(2,1)S(1)}, bf16...) custom-call(s32[1]{0:T(128)S(6)} %copy.14.count, ...), custom_call_target="tpu_custom_call" | custom-call | tf_op jit(solution)/shard_map/lean_exchange/pallas_call | solution.py:710
  143.8 13.2 %conditional.1 = (bf16[16,32,128]{2,1,0:T(8,128)(2,1)S(1)}) conditional(s32[]{:T(128)} %bitcast.5, (bf16[4,2,4,4,2,256,128]{6,5,4,3,2,1,0:T(8,128)(2,1)}, f32[128]{0:T(128)}, s32[1]{0:T(128)}, s32[160]{0:T(256)S(1)}, s32[160]{0:T(256)}, /*index=5*/bf16[160,256,256]{2,1,0:T(8,128)(2,1)}, bf16[16,32,128]{2,1,0:T(8,128)(2,1)}, s32[16,32]{1,0:T(8,128)}, ...), branch_computations={%region_0.0_spmd, %region_1.0_spmd} | conditional | bytes 8 | solution.py:878
  143.8 13.2 %remap.2 = bf16[16,32,128]{2,1,0:T(8,128)(2,1)S(1)} custom-call(s32[1]{0:T(128)} %get-tuple-element.52.count, s32[160]{0:T(256)S(1)} %get-tuple-element.53.slots, s32[160]{0:T(256)} %get-tuple-element.54.targets, bf16[160,256,256]{2,1,0:T(8,128)(2,1)} %get-tuple-element.55.weight, bf16[256,256,128]{2,1,0:T(8,128)(2,1)} %bitcast.6, ...), custom_call_target="tpu_custom_call" | custom-call | tf_op jit(solution)/shard_map/cond/branch_0_fun/remap/pallas_call | solution.py:849
  157.0 0.0 copy-start
  157.0 0.6 copy-done
Async XLA Ops:
  157.0 0.7 copy-start
